TPU v7x, 32 devices: a whole 2x2x4 slice. The times are simulated.
32 devices in a mesh: band: 8 (over y, x, core), lev: 4 (over z).
Axes of the slice: x: 2, y: 2, z: 4, core: 2. Of those that a mesh axis runs over, the one named last changes fastest.
Arguments:
- increment: bfloat16 [32, 768, 1536], P('lev', 'band'), may hold values from -6 to 6
- background: float32 [384, 2, 32, 769], P(('band', 'lev')), may hold values from -6 to 6
- legendre: bfloat16 [384, 768, 769], P(('band', 'lev')), may hold values from -6 to 6, as said below
- coupling: float32 [4, 32, 32], replicated, may hold values from -1 to 1
- damping: float32 [4], replicated, may hold values from 0.5 to 4
- target_mass: float32 [1], replicated, may hold values from 1 to 4
- numerators: int32 [4], replicated, may hold values from 8 to 32
- pair_low: int32 [384], replicated, may hold values from 0 to 383, as said below
- lat_map: int32 [768], replicated, may hold values from 0 to 767, each once
Outputs:
- analysis: bfloat16 [32, 768, 1536], P('lev', 'band')
- corrections: float32 [4], replicated
Inputs may be any that keep to these rules, and one draw needn't show every extreme that they name: Slot p holds the wavenumbers pair_low[p] and 767 - pair_low[p]; every value appears once. For the slot p with pair_low[p] = 0, legendre[p, j, 0] = 1 at every latitude j. Stored grid row r lies on latitude lat_map[r]; every latitude appears once.
All inputs are finite; a program needn't handle non-finite values.
Results may differ from a plain program's by a relative error of at most 0.0078.
Values may be sent and summed in bfloat16 or wider, within the bound.
A program may use at most 128 MiB of HBM per device.

v0:
```python
import math

import jax
import jax.numpy as jnp
from jax import lax
from jax.experimental import pallas as pl
from jax.experimental.pallas import tpu as pltpu
from jax.sharding import PartitionSpec as P

NT = 767
NLAT = 768
NLON = 1536
LEV = 32
STEPS = 4
DEN = 64
NPAIR = 384
AXES = ("band", "lev")


def wave_table(pair_low):
    column = jnp.arange(4 * pair_low.shape[0], dtype=jnp.int32)
    low = jnp.repeat(pair_low, 4)
    wavenumber = jnp.where(column // 2 % 2 == 0, low, NT - low)[:, None]
    quarter = (column % 2 * (NLON // 4))[:, None]
    fine = math.gcd(128, NLON)
    unit = 2.0 * math.pi / NLON
    coarse_pts = jnp.arange(NLON // fine, dtype=jnp.int32)[None, :] * fine
    coarse = ((wavenumber * coarse_pts + quarter) % NLON).astype(jnp.float32) * unit
    rest = (wavenumber * jnp.arange(fine, dtype=jnp.int32)[None, :] % NLON).astype(
        jnp.float32
    ) * unit
    norm = math.sqrt(2.0 / NLON)
    cos_a, sin_a, cos_b, sin_b = lax.optimization_barrier(
        (jnp.cos(coarse) * norm, jnp.sin(coarse) * norm, jnp.cos(rest), jnp.sin(rest))
    )
    blocks = [
        cos_a[:, i : i + 1] * cos_b - sin_a[:, i : i + 1] * sin_b for i in range(NLON // fine)
    ]
    return jnp.concatenate(blocks, axis=1).astype(jnp.bfloat16)


def lat_weights(lat_rows):
    return jnp.cos(math.pi * ((lat_rows.astype(jnp.float32) + 0.5) / NLAT - 0.5))


def degrees(low_wave):
    columns = jnp.arange(NT + 2, dtype=jnp.int32)
    in_second = columns[None, :] >= NT + 1 - low_wave[:, None]
    degree = jnp.where(in_second, columns[None, :] - 1, low_wave[:, None] + columns[None, :])
    return (degree.astype(jnp.float32), in_second)


def body_general(
    increment, background, legendre, coupling, damping, target_mass, numerators, pair_low, lat_map
):
    band_count = lax.axis_size("band")
    lev_count = lax.axis_size("lev")
    device_count = band_count * lev_count
    band_id = lax.axis_index("band")
    lev_id = lax.axis_index("lev")
    lev_dev = increment.shape[0]
    lat_dev = increment.shape[1]
    pair_dev = legendre.shape[0]
    points = lev_dev * lat_dev
    fourier_tab = wave_table(pair_low)
    local_lats = lax.dynamic_slice_in_dim(lat_map, band_id * lat_dev, lat_dev)
    row_weight = lat_weights(local_lats)
    all_levels = 1.0 + 2.0 * jnp.arange(LEV, dtype=jnp.float32) / (LEV - 1)
    normaliser = (
        jnp.sum(all_levels) * jnp.sum(lat_weights(jnp.arange(NLAT, dtype=jnp.int32))) * NLON
    )
    fix_scale = math.sqrt(NT * NLON) / 2.0
    own_pairs = lax.dynamic_slice_in_dim(
        pair_low, (band_id * lev_count + lev_id) * pair_dev, pair_dev
    )
    degree, in_second = degrees(own_pairs)
    holder = (own_pairs == 0).astype(jnp.float32)

    fourier = jnp.einsum(
        "ck,xk->cx",
        fourier_tab,
        increment.reshape(points, NLON),
        preferred_element_type=jnp.float32,
    )
    fourier = (fourier * jnp.tile(row_weight, lev_dev)[None, :]).astype(jnp.bfloat16)
    received = lax.all_to_all(
        fourier.reshape(device_count, pair_dev * 4, points), AXES, split_axis=0, concat_axis=0
    )

    pick = (lat_map[:, None] == jnp.arange(NLAT, dtype=jnp.int32)[None, :]).astype(jnp.bfloat16)
    stored = jnp.einsum(
        "jn,pnc->pjc", pick, legendre, preferred_element_type=jnp.float32
    ).astype(jnp.bfloat16)

    received = received.reshape(band_count, lev_count, pair_dev * 4, lev_dev, lat_dev)
    waves_in = received.transpose(2, 1, 3, 0, 4).reshape(pair_dev, 4 * LEV, NLAT)
    coeffs = jnp.einsum("prj,pjc->prc", waves_in, stored, preferred_element_type=jnp.float32)
    coeffs = coeffs.reshape(pair_dev, 2, 2, LEV, NT + 2) * math.sqrt(2.0 / NLAT)
    second_cols = in_second[:, None, None, :]
    smoothing = 1.0 / (1.0 + (degree / NT) ** 4)
    incr_spec = jnp.where(second_cols, coeffs[:, 1], coeffs[:, 0]) * smoothing[:, None, None, :]
    shape_term = degree * (degree + 1.0) / (NT * (NT + 1.0))

    spectral = background
    means = []
    arrived = []
    for step_idx in range(STEPS):
        coupled = 0.7 * spectral + 0.4 * jnp.einsum(
            "lm,prmc->prlc", coupling[step_idx], spectral, precision=lax.Precision.HIGHEST
        )
        weight_now = numerators[step_idx].astype(jnp.float32) / DEN
        spectral = (
            coupled / (1.0 + damping[step_idx] * shape_term)[:, None, None, :]
            + weight_now * incr_spec
        )
        means.append(jnp.sum(spectral[:, 0, :, 0] * holder[:, None], axis=0))
        spec_bf = spectral.astype(jnp.bfloat16)
        zeros_bf = jnp.zeros_like(spec_bf)
        split_rows = jnp.stack(
            [jnp.where(second_cols, zeros_bf, spec_bf), jnp.where(second_cols, spec_bf, zeros_bf)],
            axis=1,
        )
        waves_f = jnp.einsum(
            "prc,pjc->prj",
            split_rows.reshape(pair_dev, 4 * LEV, NT + 2),
            stored,
            preferred_element_type=jnp.float32,
        )
        waves_bf = (waves_f * math.sqrt(2.0 / NT)).astype(jnp.bfloat16)
        outgoing = waves_bf.reshape(pair_dev * 4, lev_count, lev_dev, band_count, lat_dev)
        outgoing = outgoing.transpose(3, 1, 0, 2, 4).reshape(device_count, pair_dev * 4, points)
        spectral, outgoing = lax.optimization_barrier((spectral, outgoing))
        arrived.append(lax.all_to_all(outgoing, AXES, split_axis=0, concat_axis=0))

    tops, sums = [], []
    for step_idx in range(STEPS):
        grid_now = jnp.einsum(
            "cx,ck->xk",
            arrived[step_idx].reshape(NPAIR * 4, points),
            fourier_tab,
            preferred_element_type=jnp.float32,
        ).reshape(lev_dev, lat_dev, NLON)
        top = jnp.max(grid_now, axis=(1, 2))
        tops.append(top)
        sums.append(
            jnp.sum(
                jnp.sum(jnp.exp(grid_now - top[:, None, None]), axis=2) * row_weight[None, :],
                axis=1,
            )
        )

    packed = jnp.concatenate(
        [jnp.stack(tops).reshape(-1), jnp.stack(sums).reshape(-1), jnp.stack(means).reshape(-1)]
    )
    gathered = lax.all_to_all(
        jnp.broadcast_to(packed[None, :], (device_count, packed.shape[0])),
        AXES,
        split_axis=0,
        concat_axis=0,
    )
    count = STEPS * lev_dev
    all_tops = gathered[:, :count].reshape(band_count, lev_count, STEPS, lev_dev)
    all_sums = gathered[:, count : 2 * count].reshape(band_count, lev_count, STEPS, lev_dev)
    all_tops = all_tops.transpose(2, 0, 1, 3).reshape(STEPS, band_count, LEV)
    all_sums = all_sums.transpose(2, 0, 1, 3).reshape(STEPS, band_count, LEV)
    all_means = jnp.sum(gathered[:, 2 * count :], axis=0).reshape(STEPS, LEV)

    table_entry = jnp.full((), math.sqrt(2.0 / NLON), jnp.bfloat16).astype(jnp.float32)
    to_grid = math.sqrt(2.0 / NT) * table_entry
    carried = jnp.zeros((LEV,), jnp.float32)
    shift = jnp.zeros((LEV,), jnp.float32)
    fix_list = []
    for step_idx in range(STEPS):
        carried = 0.7 * carried + 0.4 * jnp.sum(coupling[step_idx] * carried[None, :], axis=1)
        base = all_means[step_idx]
        moved = (base + carried).astype(jnp.bfloat16).astype(jnp.float32) - base.astype(
            jnp.bfloat16
        ).astype(jnp.float32)
        shift = moved * to_grid
        total = jnp.sum(
            jnp.exp(all_tops[step_idx] + shift[None, :]) * all_sums[step_idx] * all_levels[None, :]
        )
        mass_fix = jnp.log(target_mass[0] / (total / normaliser))
        fix_list.append(mass_fix)
        carried = carried + mass_fix * fix_scale
    own_shift = lax.dynamic_slice_in_dim(shift, lev_id * lev_dev, lev_dev)
    analysis = (grid_now + own_shift[:, None, None]).astype(jnp.bfloat16)
    return (analysis, jnp.stack(fix_list))


GROUP = 4
MESH = pl.DeviceIdType.MESH
LAST = (((1,), (1,)), ((), ()))


def flat_dot(a, b):
    return jnp.dot(a, b, preferred_element_type=jnp.float32)


def exchange_kernel(
    sizes,
    weight_ref,
    target_ref,
    inc_ref,
    leg_ref,
    back_ref,
    cos_a_ref,
    sin_a_ref,
    cos_b_ref,
    sin_b_ref,
    cos_at_ref,
    sin_at_ref,
    cos_bt_ref,
    sin_bt_ref,
    rows_ref,
    lat_ref,
    consts_ref,
    mix_ref,
    grid_ref,
    fix_ref,
    shift_ref,
    points_in,
    table,
    table_t,
    pick,
    leg_buf,
    stored,
    back_buf,
    incr,
    spec,
    turn,
    acc,
    send,
    recv,
    means,
    stat_send,
    stat_recv,
    load_sem,
    leg_sem,
    back_sem,
    send_sem,
    recv_sem,
    stat_sem,
    out_sem,
):
    bands, levs, lev_dev, lat_dev, chunks = sizes
    devs = bands * levs
    band_id = lax.axis_index("band")
    lev_id = lax.axis_index("lev")
    me = band_id * levs + lev_id
    piece = 32
    splits = lat_dev // piece
    rows = 4 * GROUP
    cols = devs * rows
    points = lev_dev * lat_dev
    slots = chunks * GROUP
    per_tile = 128 // piece
    halves = lev_dev // per_tile

    barrier = pltpu.get_barrier_semaphore()

    def peer(o):
        return (
            lax.rem(band_id + lax.rem(o, bands), bands),
            lax.rem(lev_id + o // bands, levs),
        )

    def greet(o, _):
        pl.semaphore_signal(barrier, inc=1, device_id=peer(o), device_id_type=MESH)
        return 0

    lax.fori_loop(1, devs, greet, 0)

    def load_piece(i, j):
        return pltpu.make_async_copy(
            inc_ref.at[i, pl.ds(j * piece, piece), :],
            points_in.at[pl.ds((j * lev_dev + i) * piece, piece), :],
            load_sem,
        )

    for j in range(splits):
        for i in range(lev_dev):
            load_piece(i, j).start()

    def leg_copy(slot):
        return pltpu.make_async_copy(
            leg_ref.at[slot], leg_buf.at[lax.rem(slot, 2)], leg_sem.at[lax.rem(slot, 2)]
        )

    def back_copy(slot):
        return pltpu.make_async_copy(
            back_ref.at[slot], back_buf.at[lax.rem(slot, 2)], back_sem.at[lax.rem(slot, 2)]
        )

    for slot in range(2):
        leg_copy(slot).start()
        back_copy(slot).start()

    def message(t, o):
        db, dz = peer(o)
        return pltpu.make_async_remote_copy(
            src_ref=send.at[t, pl.ds((db * levs + dz) * rows, rows), :],
            dst_ref=recv.at[t, pl.ds(me * rows, rows), :],
            send_sem=send_sem.at[t],
            recv_sem=recv_sem.at[t],
            device_id=(db, dz),
            device_id_type=MESH,
        )

    def send_all(t):
        def one(o, _):
            message(t, o).start()
            return 0

        lax.fori_loop(1, devs, one, 0)
        pltpu.make_async_copy(
            send.at[t, pl.ds(me * rows, rows), :],
            recv.at[t, pl.ds(me * rows, rows), :],
            recv_sem.at[t],
        ).start()

    def wait_recv(t):
        pltpu.make_async_copy(recv.at[t], recv.at[t], recv_sem.at[t]).wait()

    row_weight = rows_ref[...]

    def fourier(ch, _):
        def fill(rb, _):
            base = pl.multiple_of(ch * cols + rb * 128, 128)
            out = pl.multiple_of(rb * 128, 128)
            cos_b = cos_b_ref[pl.ds(base, 128), :]
            sin_b = sin_b_ref[pl.ds(base, 128), :]
            cos_a = cos_a_ref[pl.ds(base, 128), :]
            sin_a = sin_a_ref[pl.ds(base, 128), :]
            for kc in range(NLON // 128):
                table[pl.ds(out, 128), kc * 128 : (kc + 1) * 128] = (
                    cos_a[:, kc : kc + 1] * cos_b - sin_a[:, kc : kc + 1] * sin_b
                ).astype(jnp.bfloat16)
            return 0

        lax.fori_loop(0, cols // 128, fill, 0)

        @pl.when(ch == 0)
        def _():
            pltpu.make_async_copy(points_in, points_in, load_sem).wait()

        got = lax.dot_general(
            table[...], points_in[...], LAST, preferred_element_type=jnp.float32
        )
        send[ch] = (got * row_weight).astype(jnp.bfloat16)

        @pl.when(ch == 0)
        def _():
            pl.semaphore_wait(barrier, devs - 1)

        send_all(ch)
        return 0

    lax.fori_loop(0, chunks, fourier, 0)

    def fill_t(kc, _):
        cos_a = cos_at_ref[pl.ds(kc, 1), :]
        sin_a = sin_at_ref[pl.ds(kc, 1), :]
        table_t[pl.ds(pl.multiple_of(kc * 128, 128), 128), :] = (
            cos_a * cos_bt_ref[...] - sin_a * sin_bt_ref[...]
        ).astype(jnp.bfloat16)
        return 0

    lax.fori_loop(0, NLON // 128, fill_t, 0)
    pick[...] = (
        (lat_ref[...] == lax.broadcasted_iota(jnp.int32, (NLAT, NLAT), 1))
        .astype(jnp.float32)
        .astype(jnp.bfloat16)
    )
    means[...] = jnp.zeros_like(means)
    lane_part = lax.broadcasted_iota(jnp.int32, (rows, 128), 1) // piece

    def gather_pieces(parts):
        out = parts[0]
        for n in range(1, per_tile):
            out = jnp.where(lane_part == n, parts[n], out)
        return out

    def rolled(x, amount):
        amount = amount * piece % 128
        return pltpu.roll(x, amount, 1) if amount else x

    def chunk_body(ch, _):
        def prepare(s, _):
            slot = ch * GROUP + s
            leg_copy(slot).wait()
            stored[s] = flat_dot(pick[...], leg_buf[lax.rem(slot, 2)]).astype(jnp.bfloat16)

            @pl.when(slot + 2 < slots)
            def _():
                leg_copy(slot + 2).start()

            return 0

        lax.fori_loop(0, GROUP, prepare, 0)
        wait_recv(ch)

        def arrive(z, _):
            for half in range(halves):
                for t in range(NLAT // 128):
                    tiles = []
                    for n in range(per_tile):
                        g = t * per_tile + n
                        b, j = g // splits, g % splits
                        lane0 = (j * halves + half) * 128
                        tiles.append(
                            recv[
                                ch,
                                pl.ds(pl.multiple_of((b * levs + z) * rows, rows), rows),
                                lane0 : lane0 + 128,
                            ].astype(jnp.float32)
                        )
                    for il in range(per_tile):
                        level = z * lev_dev + half * per_tile + il
                        turn[t, pl.ds(pl.multiple_of(level * rows, rows), rows), :] = gather_pieces([rolled(tiles[n], n - il) for n in range(per_tile)])
            return 0

        lax.fori_loop(0, levs, arrive, 0)

        def direct(s, _):
            slot = ch * GROUP + s
            back_copy(slot).wait()
            waves_in = jnp.concatenate(
                [
                    jnp.concatenate(
                        [
                            turn[t, pl.ds(s * 4 + qr, LEV, stride=rows), :]
                            for t in range(NLAT // 128)
                        ],
                        axis=1,
                    )
                    for qr in range(4)
                ],
                axis=0,
            ).astype(jnp.bfloat16)
            coeffs = flat_dot(waves_in, stored[s]) * math.sqrt(2.0 / NLAT)
            second = consts_ref[slot, 0:1, :] > 0.5
            incr[s] = (
                jnp.where(second, coeffs[2 * LEV :], coeffs[: 2 * LEV]) * consts_ref[slot, 1:2, :]
            )
            spec[s] = back_buf[lax.rem(slot, 2)]

            @pl.when(slot + 2 < slots)
            def _():
                back_copy(slot + 2).start()

            return 0

        lax.fori_loop(0, GROUP, direct, 0)

        def step(k, _):
            def inverse(s, _):
                slot = ch * GROUP + s
                second = consts_ref[slot, 0:1, :] > 0.5
                inv = consts_ref[slot, pl.ds(2 + k, 1), :]
                mix = mix_ref[k][:, :LEV]
                now = [
                    jnp.dot(
                        mix,
                        spec[s, r * LEV : (r + 1) * LEV, :],
                        precision=lax.Precision.HIGHEST,
                        preferred_element_type=jnp.float32,
                    )
                    * inv
                    + weight_ref[k] * incr[s, r * LEV : (r + 1) * LEV, :]
                    for r in range(2)
                ]
                for r in range(2):
                    spec[s, r * LEV : (r + 1) * LEV, :] = now[r]
                means[k] += now[0][:, :128] * consts_ref[slot, 6:7, :128]
                both = jnp.concatenate(now, axis=0)
                split = jnp.concatenate(
                    [jnp.where(second, 0.0, both), jnp.where(second, both, 0.0)], axis=0
                ).astype(jnp.bfloat16)
                waves = lax.dot_general(
                    split, stored[s], LAST, preferred_element_type=jnp.float32
                ) * math.sqrt(2.0 / NT)
                for qr in range(4):
                    for t in range(NLAT // 128):
                        turn[t, pl.ds(s * 4 + qr, LEV, stride=rows), :] = waves[
                            qr * LEV : (qr + 1) * LEV, t * 128 : (t + 1) * 128
                        ]
                return 0

            lax.fori_loop(0, GROUP, inverse, 0)
            t_out = chunks + ch * STEPS + k

            def depart(z, _):
                for half in range(halves):
                    for t in range(NLAT // 128):
                        tiles = []
                        for il in range(per_tile):
                            level = z * lev_dev + half * per_tile + il
                            tiles.append(
                                turn[t, pl.ds(pl.multiple_of(level * rows, rows), rows), :]
                            )
                        for n in range(per_tile):
                            g = t * per_tile + n
                            b, j = g // splits, g % splits
                            lane0 = (j * halves + half) * 128
                            send[
                                t_out,
                                pl.ds(pl.multiple_of((b * levs + z) * rows, rows), rows),
                                lane0 : lane0 + 128,
                            ] = gather_pieces(
                                [rolled(tiles[il], il - n) for il in range(per_tile)]
                            ).astype(jnp.bfloat16)
                return 0

            lax.fori_loop(0, levs, depart, 0)
            send_all(t_out)
            return 0

        lax.fori_loop(0, STEPS, step, 0)
        return 0

    lax.fori_loop(0, chunks, chunk_body, 0)

    wide = 256
    sub = lax.broadcasted_iota(jnp.int32, (lev_dev, points), 0)
    in_level = lax.broadcasted_iota(jnp.int32, (lev_dev, points), 1) // piece % lev_dev == sub
    lane = lax.broadcasted_iota(jnp.int32, (lev_dev, 128), 1)
    own_lane = lev_id * lev_dev + lax.broadcasted_iota(jnp.int32, (lev_dev, 128), 0)
    low = -1e30

    def grid_part(k, lo, hi, add):
        def part(nb, _):
            at = pl.ds(pl.multiple_of(nb * wide, wide), wide)
            total = None
            for ch in range(lo, hi):
                one = flat_dot(
                    table_t[:, ch * cols : (ch + 1) * cols], recv[chunks + ch * STEPS + k, :, at]
                )
                total = one if total is None else total + one
            acc[:, at] = acc[:, at] + total if add else total
            return 0

        lax.fori_loop(0, points // wide, part, 0)

    def mass(k, tops_row, sums_row):
        tops, sums = [], []
        for nb in range(points // wide):
            tile = acc[:, nb * wide : (nb + 1) * wide]
            top = jnp.max(tile, axis=0, keepdims=True)
            tops.append(top)
            sums.append(jnp.sum(jnp.exp(tile - top), axis=0, keepdims=True))
        top = jnp.concatenate(tops, axis=1)
        total = jnp.concatenate(sums, axis=1) * row_weight
        level_top = jnp.max(jnp.where(in_level, top, low), axis=1, keepdims=True)
        level_sum = jnp.sum(
            jnp.where(in_level, total * jnp.exp(jnp.minimum(top - level_top, 0.0)), 0.0),
            axis=1,
            keepdims=True,
        )
        here = lane == own_lane + LEV * k
        tops_row = jnp.where(
            jnp.max(here.astype(jnp.float32), axis=0, keepdims=True) > 0.5,
            jnp.sum(jnp.where(here, level_top, 0.0), axis=0, keepdims=True),
            tops_row,
        )
        sums_row = sums_row + jnp.sum(jnp.where(here, level_sum, 0.0), axis=0, keepdims=True)
        return tops_row, sums_row

    def early(k, carry):
        def take(ch, _):
            wait_recv(chunks + ch * STEPS + k)
            return 0

        lax.fori_loop(0, chunks, take, 0)
        grid_part(k, 0, chunks, False)
        return mass(k, *carry)

    rows_now = (jnp.full((1, 128), low, jnp.float32), jnp.zeros((1, 128), jnp.float32))
    rows_now = lax.fori_loop(0, STEPS - 1, early, rows_now)
    k = STEPS - 1
    if chunks > 1:
        for ch in range(chunks - 1):
            wait_recv(chunks + ch * STEPS + k)
        grid_part(k, 0, chunks - 1, False)
    wait_recv(chunks + (chunks - 1) * STEPS + k)
    grid_part(k, chunks - 1, chunks, chunks > 1)
    grid_out = pltpu.make_async_copy(acc, grid_ref, out_sem)
    grid_out.start()
    tops_row, sums_row = mass(k, *rows_now)

    wide_lane = lax.broadcasted_iota(jnp.int32, (LEV, 128), 1)
    diag = lax.broadcasted_iota(jnp.int32, (LEV, 128), 0)
    means_row = jnp.zeros((1, 128), jnp.float32)
    for n in range(STEPS):
        column = jnp.sum(jnp.where(wide_lane == 0, means[n], 0.0), axis=1, keepdims=True)
        means_row = means_row + jnp.sum(
            jnp.where(wide_lane == diag + LEV * n, column, 0.0), axis=0, keepdims=True
        )
    stat_send[0:1, :] = tops_row
    stat_send[1:2, :] = sums_row
    stat_send[2:3, :] = means_row
    stat_send[3:4, :] = jnp.zeros((1, 128), jnp.float32)

    def stat_one(o, _):
        db, dz = peer(o)
        pltpu.make_async_remote_copy(
            src_ref=stat_send,
            dst_ref=stat_recv.at[me],
            send_sem=stat_sem.at[0],
            recv_sem=stat_sem.at[1],
            device_id=(db, dz),
            device_id_type=MESH,
        ).start()
        return 0

    lax.fori_loop(1, devs, stat_one, 0)
    pltpu.make_async_copy(stat_send, stat_recv.at[me], stat_sem.at[1]).start()

    def finish(t, _):
        left = send.at[t, pl.ds(0, (devs - 1) * rows), :]
        pltpu.make_async_copy(left, left, send_sem.at[t]).wait()
        return 0

    lax.fori_loop(0, chunks * (1 + STEPS), finish, 0)
    pltpu.make_async_copy(stat_recv, stat_recv, stat_sem.at[1]).wait()

    def find_top(d, best):
        return jnp.maximum(best, stat_recv[d, 0:1, :])

    best = lax.fori_loop(0, devs, find_top, jnp.full((1, 128), low, jnp.float32))

    def add_up(d, carry):
        total, base = carry
        return (
            total + stat_recv[d, 1:2, :] * jnp.exp(stat_recv[d, 0:1, :] - best),
            base + stat_recv[d, 2:3, :],
        )

    zero_row = jnp.zeros((1, 128), jnp.float32)
    total, base = lax.fori_loop(0, devs, add_up, (zero_row, zero_row))

    lane8 = lax.broadcasted_iota(jnp.int32, (8, 128), 1)
    is_level = lane8 < LEV
    level_weight = jnp.where(
        is_level, 1.0 + 2.0 * lane8.astype(jnp.float32) / (LEV - 1), 0.0
    )
    to_grid = target_ref[1]
    normaliser = target_ref[2]
    fix_scale = math.sqrt(NT * NLON) / 2.0
    best = jnp.broadcast_to(best, (8, 128))
    total = jnp.broadcast_to(total, (8, 128))
    base = jnp.broadcast_to(base, (8, 128))
    carried = jnp.zeros((8, 128), jnp.float32)
    shift = carried
    fixes = carried
    for n in range(STEPS):
        back = (128 - LEV * n) % 128
        best_n, total_n, base_n = [
            pltpu.roll(x, back, 1) if back else x for x in (best, total, base)
        ]
        column = jnp.sum(mix_ref[n] * carried[0:1], axis=1, keepdims=True)
        moved_by = jnp.broadcast_to(
            jnp.sum(jnp.where(wide_lane == diag, column, 0.0), axis=0, keepdims=True), (8, 128)
        )
        moved = (base_n + moved_by).astype(jnp.bfloat16).astype(jnp.float32) - base_n.astype(
            jnp.bfloat16
        ).astype(jnp.float32)
        shift = jnp.where(is_level, moved * to_grid, 0.0)
        mass_n = jnp.sum(
            jnp.where(
                is_level, jnp.exp(jnp.where(is_level, best_n + shift, 0.0)) * total_n, 0.0
            )
            * level_weight,
            axis=1,
            keepdims=True,
        )
        fix = jnp.log(target_ref[0] / (mass_n / normaliser))
        fixes = jnp.where(lane8 == n, fix, fixes)
        carried = jnp.where(is_level, moved_by + fix * fix_scale, 0.0)
    fix_ref[...] = fixes
    own = jnp.sum(jnp.where(lane == own_lane, shift[0:1], 0.0), axis=1, keepdims=True)
    shift_ref[...] = jnp.broadcast_to(own, (lev_dev, 128))

    pltpu.make_async_copy(
        stat_recv.at[pl.ds(0, devs - 1)], stat_recv.at[pl.ds(0, devs - 1)], stat_sem.at[0]
    ).wait()
    grid_out.wait()


def finish_kernel(shift_ref, grid_ref, out_ref):
    first = pl.program_id(0) * out_ref.shape[0]
    turned = grid_ref[...].T
    for n in range(out_ref.shape[0]):
        out_ref[n, 0] = (
            turned[n * 32 : (n + 1) * 32] + shift_ref[pl.ds(first + n, 1), 0:1]
        ).astype(jnp.bfloat16)


def table_factors(wavenumber, quarter, points, axis):
    phase = (wavenumber * points + quarter) % NLON
    angle = phase.astype(jnp.float32) * (2.0 * math.pi / NLON)
    return jnp.cos(angle), jnp.sin(angle)


def body(
    increment, background, legendre, coupling, damping, target_mass, numerators, pair_low, lat_map
):
    band_count = lax.axis_size("band")
    lev_count = lax.axis_size("lev")
    devs = band_count * lev_count
    lev_dev, lat_dev = increment.shape[:2]
    pair_dev = legendre.shape[0]
    points = lev_dev * lat_dev
    cols = devs * 4 * GROUP
    fits = (
        lat_dev % 32 == 0
        and pair_dev % GROUP == 0
        and lev_dev == 8
        and points % 256 == 0
        and LEV * STEPS == 128
    )
    if not fits:
        return body_general(
            increment,
            background,
            legendre,
            coupling,
            damping,
            target_mass,
            numerators,
            pair_low,
            lat_map,
        )
    chunks = pair_dev // GROUP
    band_id = lax.axis_index("band")
    lev_id = lax.axis_index("lev")

    low = pair_low.reshape(devs, chunks, GROUP).transpose(1, 0, 2).reshape(-1)
    column = jnp.arange(4 * low.shape[0], dtype=jnp.int32)
    wave = jnp.repeat(low, 4)
    wave = jnp.where(column // 2 % 2 == 0, wave, NT - wave)
    quarter = column % 2 * (NLON // 4)
    coarse = jnp.arange(NLON // 128, dtype=jnp.int32) * 128
    fine = jnp.arange(128, dtype=jnp.int32)
    norm = math.sqrt(2.0 / NLON)
    cos_a, sin_a = table_factors(wave[:, None], quarter[:, None], coarse[None, :], 1)
    cos_b, sin_b = table_factors(wave[:, None], 0, fine[None, :], 1)
    cos_a, sin_a = cos_a * norm, sin_a * norm
    cos_at, sin_at = table_factors(wave[None, :], quarter[None, :], coarse[:, None], 0)
    cos_bt, sin_bt = table_factors(wave[None, :], 0, fine[:, None], 0)
    cos_at, sin_at = cos_at * norm, sin_at * norm

    local_lats = lax.dynamic_slice_in_dim(lat_map, band_id * lat_dev, lat_dev)
    row_weight = lat_weights(local_lats).reshape(lat_dev // 32, 1, 32)
    row_weight = jnp.broadcast_to(row_weight, (lat_dev // 32, lev_dev, 32)).reshape(1, points)
    own_pairs = lax.dynamic_slice_in_dim(
        pair_low, (band_id * lev_count + lev_id) * pair_dev, pair_dev
    )
    degree, in_second = degrees(own_pairs)
    holder = jnp.broadcast_to((own_pairs == 0).astype(jnp.float32)[:, None], degree.shape)
    shape_term = degree * (degree + 1.0) / (NT * (NT + 1.0))
    consts = jnp.stack(
        [in_second.astype(jnp.float32), 1.0 / (1.0 + (degree / NT) ** 4)]
        + [1.0 / (1.0 + damping[n] * shape_term) for n in range(STEPS)]
        + [holder, holder],
        axis=1,
    )
    eye = jnp.eye(LEV, dtype=jnp.float32)
    mix = jnp.pad(0.7 * eye + 0.4 * coupling, ((0, 0), (0, 0), (0, 128 - LEV)))
    all_levels = 1.0 + 2.0 * jnp.arange(LEV, dtype=jnp.float32) / (LEV - 1)
    normaliser = (
        jnp.sum(all_levels) * jnp.sum(lat_weights(jnp.arange(NLAT, dtype=jnp.int32))) * NLON
    )
    table_entry = jnp.full((), norm, jnp.bfloat16).astype(jnp.float32)
    scalars = jnp.stack([target_mass[0], math.sqrt(2.0 / NT) * table_entry, normaliser])
    weights = numerators.astype(jnp.float32) / DEN

    vmem = pl.BlockSpec(memory_space=pltpu.VMEM)
    smem = pl.BlockSpec(memory_space=pltpu.SMEM)
    hbm = pl.BlockSpec(memory_space=pl.ANY)
    total = chunks * (1 + STEPS)
    dma = pltpu.SemaphoreType.DMA
    grid_t, fixes, shift = pl.pallas_call(
        lambda *refs: exchange_kernel(
            (band_count, lev_count, lev_dev, lat_dev, chunks), *refs
        ),
        out_shape=(
            jax.ShapeDtypeStruct((NLON, points), jnp.float32),
            jax.ShapeDtypeStruct((8, 128), jnp.float32),
            jax.ShapeDtypeStruct((lev_dev, 128), jnp.float32),
        ),
        in_specs=[smem, smem, hbm, hbm, hbm] + [vmem] * 12,
        out_specs=(hbm, vmem, vmem),
        scratch_shapes=[
            pltpu.VMEM((points, NLON), jnp.bfloat16),
            pltpu.VMEM((cols, NLON), jnp.bfloat16),
            pltpu.VMEM((NLON, chunks * cols), jnp.bfloat16),
            pltpu.VMEM((NLAT, NLAT), jnp.bfloat16),
            pltpu.VMEM((2, NLAT, NT + 2), jnp.bfloat16),
            pltpu.VMEM((GROUP, NLAT, NT + 2), jnp.bfloat16),
            pltpu.VMEM((2, 2 * LEV, NT + 2), jnp.float32),
            pltpu.VMEM((GROUP, 2 * LEV, NT + 2), jnp.float32),
            pltpu.VMEM((GROUP, 2 * LEV, NT + 2), jnp.float32),
            pltpu.VMEM((NLAT // 128, LEV * 4 * GROUP, 128), jnp.float32),
            pltpu.VMEM((NLON, points), jnp.float32),
            pltpu.VMEM((total, cols, points), jnp.bfloat16),
            pltpu.VMEM((total, cols, points), jnp.bfloat16),
            pltpu.VMEM((STEPS, LEV, 128), jnp.float32),
            pltpu.VMEM((4, 128), jnp.float32),
            pltpu.VMEM((devs, 4, 128), jnp.float32),
            dma,
            dma((2,)),
            dma((2,)),
            dma((total,)),
            dma((total,)),
            dma((2,)),
            dma,
        ],
        compiler_params=pltpu.CompilerParams(
            collective_id=0, has_side_effects=True, vmem_limit_bytes=67043328
        ),
    )(
        weights,
        scalars,
        increment,
        legendre,
        background.reshape(pair_dev, 2 * LEV, NT + 2),
        cos_a,
        sin_a,
        cos_b,
        sin_b,
        cos_at,
        sin_at,
        cos_bt,
        sin_bt,
        row_weight,
        lat_map[:, None],
        consts,
        mix,
    )

    halves = lev_dev // 4
    splits = lat_dev // 32
    analysis = pl.pallas_call(
        finish_kernel,
        grid=(halves, splits),
        in_specs=[
            pl.BlockSpec((lev_dev, 128), lambda h, j: (0, 0)),
            pl.BlockSpec((NLON, 128), lambda h, j: (0, j * halves + h)),
        ],
        out_specs=pl.BlockSpec((4, 1, 32, NLON), lambda h, j: (h, j, 0, 0)),
        out_shape=jax.ShapeDtypeStruct((lev_dev, splits, 32, NLON), jnp.bfloat16),
    )(shift, grid_t)
    return (analysis.reshape(lev_dev, lat_dev, NLON), fixes[0, :STEPS])


def solution(mesh):
    return jax.shard_map(
        body,
        mesh=mesh,
        in_specs=(
            P("lev", "band", None),
            P(("band", "lev"), None, None, None),
            P(("band", "lev"), None, None),
            P(),
            P(),
            P(),
            P(),
            P(),
            P(),
        ),
        out_specs=(P("lev", "band", None), P()),
        check_vma=False,
    )
```

profile of v0, /device:TPU:0, one launch (start us, length us, event | category | flops | bytes accessed | tf_op | source)
XLA Modules:
  0.0 334.4 jit_solution(2502218754725379060)
XLA Ops:
  0.6 0.6 add_reduce_fusion
  1.2 0.6 cosine_reduce_fusion
  3.8 0.6 pad_maximum_fusion.refs_1_
  4.4 0.8 multiply_cosine_fusion
  5.3 1.2 convert_multiply_fusion.refs_0_
  6.4 0.8 compare_convert_fusion.1
  7.3 1.5 fusion.35
  11.3 0.7 reshape.527.refs_13_
  12.2 0.9 multiply_add_fusion
  13.1 0.6 pad.4.refs_16_
  13.7 0.8 reshape.524
  14.7 0.1 reshape.526
  15.0 1.2 sine_multiply_fusion.1
  16.2 0.4 add_divide_fusion
  16.6 1.2 stack.8.refs_15_
  17.8 1.7 broadcast_in_dim.18.refs_14_
  19.4 0.3 copy.16
  19.7 3.6 %sine_multiply_fusion = (f32[1536,12]{1,0:T(8,128)}, f32[1536,12]{1,0:T(8,128)}) fusion(f32[1536,12]{1,0:T(8,128)S(1)} %copy.16), kind=kLoop, calls=%fused_computation.16 | loop fusion | flops 55296 | bytes 221184 | tf_op jit(solution)/shard_map/mul | solution.py:748
  23.4 4.6 %fusion.10 = (f32[1536,128]{1,0:T(8,128)}, f32[1536,128]{1,0:T(8,128)}) fusion(s32[1536]{0:T(1024)S(1)} %get-tuple-element.27), kind=kLoop, calls=%fused_computation.14 | loop fusion | flops 1769472 | bytes 1579008 | tf_op jit(solution)/shard_map/sin | solution.py:702
  28.0 4.4 %fusion.6 = (f32[128,1536]{1,0:T(8,128)}, f32[128,1536]{1,0:T(8,128)}) fusion(s32[1536]{0:T(1024)S(1)} %get-tuple-element.27), kind=kLoop, calls=%fused_computation.9 | loop fusion | flops 1769472 | bytes 1579008 | tf_op jit(solution)/shard_map/sin | solution.py:702
  32.4 19.5 %copy.17.refs_3_ = bf16[12,768,769]{2,1,0:T(8,128)(2,1)} copy(bf16[12,768,769]{1,2,0:T(8,128)(2,1)} %param.11) | data formatting | bytes 28348416 | tf_op args[2]
  51.9 275.3 %shard_map.104 = (f32[1536,768]{1,0:T(8,128)}, f32[8,128]{1,0:T(8,128)}, f32[8,128]{1,0:T(8,128)}) custom-call(f32[4]{0:T(128)} %convert_multiply_fusion.refs_0_, f32[3]{0:T(128)} %pad_maximum_fusion.refs_1_, bf16[8,96,1536]{2,1,0:T(8,128)(2,1)} %refs_2_.1, bf16[12,768,769]{2,1,0:T(8,128)(2,1)} %copy.17.refs_3_, f32[12,64,769]{2,1,0:T(8,128)} %bitcast.10, ...), custom_call_target="tpu_custom_call" | custom-call | tf_op jit(solution)/shard_map/pallas_call | solution.py:783
  327.1 6.1 %shard_map.105 = bf16[8,3,32,1536]{3,2,1,0:T(8,128)(2,1)} custom-call(f32[8,128]{1,0:T(8,128)} %get-tuple-element.5.shift_ref, f32[1536,768]{1,0:T(8,128)} %get-tuple-element.6.grid_ref), custom_call_target="tpu_custom_call" | custom-call | tf_op jit(solution)/shard_map/pallas_call | solution.py:844
  333.2 1.2 slice_bitcast_fusion
  (13 shorter events, 0.6 us)
where the time goes:
time: 336 us; the launch traced here: 334 us
  Pallas kernels  281 us (84%)
  local copies, waits for them, and re-layouts  27.9 us (8%)
  other arithmetic  19.9 us (6%)
  between operations  5.27 us (2%)
    pallas_call x1, Pallas kernels, body(): pl.pallas_call(lambda *refs: exchange_kernel((band_count, lev_count, lev_...  275 us
    unnamed x1, local copies, waits for them, and re-layouts  19.5 us
    sin x2, other arithmetic, table_factors(): return (jnp.cos(angle), jnp.sin(angle))  9 us

commit v1 on v0

--- a/solution.py
+++ b/solution.py
@@ -1,6 +1,7 @@
 import math
 
 import jax
+import numpy as np
 import jax.numpy as jnp
 from jax import lax
 from jax.experimental import pallas as pl
@@ -193,32 +194,40 @@
 LAST = (((1,), (1,)), ((), ()))
 
 
+def sine(x):
+    y = x * x
+    out = -1.0 / math.factorial(11)
+    for n in (9, 7, 5, 3, 1):
+        out = out * y + (1.0 if n % 4 == 1 else -1.0) / math.factorial(n)
+    return out * x
+
+
+def table_values(phase):
+    turns = jnp.floor((phase + 0.5) * (1.0 / NLON))
+    rest = jnp.abs(phase - turns * NLON - NLON / 2) - NLON / 4
+    return (sine(rest * (2.0 * math.pi / NLON)) * math.sqrt(2.0 / NLON)).astype(jnp.bfloat16)
+
+
 def flat_dot(a, b):
     return jnp.dot(a, b, preferred_element_type=jnp.float32)
 
 
 def exchange_kernel(
     sizes,
-    weight_ref,
+    numer_ref,
+    damp_ref,
     target_ref,
     inc_ref,
     leg_ref,
     back_ref,
-    cos_a_ref,
-    sin_a_ref,
-    cos_b_ref,
-    sin_b_ref,
-    cos_at_ref,
-    sin_at_ref,
-    cos_bt_ref,
-    sin_bt_ref,
-    rows_ref,
+    pair_ref,
     lat_ref,
-    consts_ref,
-    mix_ref,
+    coupling_ref,
     grid_ref,
     fix_ref,
     shift_ref,
+    consts_ref,
+    mix_ref,
     points_in,
     table,
     table_t,
@@ -322,57 +331,6 @@
     def wait_recv(t):
         pltpu.make_async_copy(recv.at[t], recv.at[t], recv_sem.at[t]).wait()
 
-    row_weight = rows_ref[...]
-
-    def fourier(ch, _):
-        def fill(rb, _):
-            base = pl.multiple_of(ch * cols + rb * 128, 128)
-            out = pl.multiple_of(rb * 128, 128)
-            cos_b = cos_b_ref[pl.ds(base, 128), :]
-            sin_b = sin_b_ref[pl.ds(base, 128), :]
-            cos_a = cos_a_ref[pl.ds(base, 128), :]
-            sin_a = sin_a_ref[pl.ds(base, 128), :]
-            for kc in range(NLON // 128):
-                table[pl.ds(out, 128), kc * 128 : (kc + 1) * 128] = (
-                    cos_a[:, kc : kc + 1] * cos_b - sin_a[:, kc : kc + 1] * sin_b
-                ).astype(jnp.bfloat16)
-            return 0
-
-        lax.fori_loop(0, cols // 128, fill, 0)
-
-        @pl.when(ch == 0)
-        def _():
-            pltpu.make_async_copy(points_in, points_in, load_sem).wait()
-
-        got = lax.dot_general(
-            table[...], points_in[...], LAST, preferred_element_type=jnp.float32
-        )
-        send[ch] = (got * row_weight).astype(jnp.bfloat16)
-
-        @pl.when(ch == 0)
-        def _():
-            pl.semaphore_wait(barrier, devs - 1)
-
-        send_all(ch)
-        return 0
-
-    lax.fori_loop(0, chunks, fourier, 0)
-
-    def fill_t(kc, _):
-        cos_a = cos_at_ref[pl.ds(kc, 1), :]
-        sin_a = sin_at_ref[pl.ds(kc, 1), :]
-        table_t[pl.ds(pl.multiple_of(kc * 128, 128), 128), :] = (
-            cos_a * cos_bt_ref[...] - sin_a * sin_bt_ref[...]
-        ).astype(jnp.bfloat16)
-        return 0
-
-    lax.fori_loop(0, NLON // 128, fill_t, 0)
-    pick[...] = (
-        (lat_ref[...] == lax.broadcasted_iota(jnp.int32, (NLAT, NLAT), 1))
-        .astype(jnp.float32)
-        .astype(jnp.bfloat16)
-    )
-    means[...] = jnp.zeros_like(means)
     lane_part = lax.broadcasted_iota(jnp.int32, (rows, 128), 1) // piece
 
     def gather_pieces(parts):
@@ -385,11 +343,112 @@
         amount = amount * piece % 128
         return pltpu.roll(x, amount, 1) if amount else x
 
+    lat_now = (lat_ref[...].astype(jnp.float32) + 0.5) / NLAT - 0.5
+    lat_now = jnp.broadcast_to(sine((0.5 - jnp.abs(lat_now)) * math.pi), (rows, NLAT))
+    weight_tiles = []
+    for j in range(splits):
+        tile = jnp.zeros((rows, 128), jnp.float32)
+        for b in range(bands):
+            t, n = (b * splits + j) // per_tile, (b * splits + j) % per_tile
+            source = lat_now[:, t * 128 : (t + 1) * 128]
+            part = gather_pieces([rolled(source, il - n) for il in range(per_tile)])
+            tile = jnp.where(band_id == b, part, tile)
+        weight_tiles += [tile] * halves
+    row_weight = jnp.concatenate(weight_tiles, axis=1)[0:1]
+    pairs = pair_ref[...].astype(jnp.float32)
+    pair_count = pairs.shape[1]
+    pair_dev = chunks * GROUP
+
+    def fourier(ch, _):
+        def fill(rb, _):
+            col = rb * 128 + lax.broadcasted_iota(jnp.int32, (128, 1), 0)
+            place = (col >> 4) * pair_dev + ch * GROUP + ((col & 15) >> 2)
+            spot = lax.broadcasted_iota(jnp.int32, (128, pair_count), 1) == place
+            wave = jnp.sum(jnp.where(spot, pairs, 0.0), axis=1, keepdims=True)
+            wave = jnp.where((col & 2) == 0, wave, NT - wave)
+            wave = jnp.broadcast_to(wave, (128, 128))
+            quarter = ((col & 1) * (NLON // 4)).astype(jnp.float32)
+            lanes = lax.broadcasted_iota(jnp.int32, (1, 128), 1).astype(jnp.float32)
+            out = pl.multiple_of(rb * 128, 128)
+            for kc in range(NLON // 128):
+                table[pl.ds(out, 128), kc * 128 : (kc + 1) * 128] = table_values(
+                    wave * (lanes + kc * 128.0) + quarter
+                )
+            return 0
+
+        lax.fori_loop(0, cols // 128, fill, 0)
+
+        @pl.when(ch == 0)
+        def _():
+            pltpu.make_async_copy(points_in, points_in, load_sem).wait()
+
+        got = lax.dot_general(
+            table[...], points_in[...], LAST, preferred_element_type=jnp.float32
+        )
+        send[ch] = (got * row_weight).astype(jnp.bfloat16)
+
+        @pl.when(ch == 0)
+        def _():
+            pl.semaphore_wait(barrier, devs - 1)
+
+        send_all(ch)
+        return 0
+
+    lax.fori_loop(0, chunks, fourier, 0)
+
+    same = lax.broadcasted_iota(jnp.int32, (pair_count, pair_count), 0) == (
+        lax.broadcasted_iota(jnp.int32, (pair_count, pair_count), 1)
+    )
+    pair_column = jnp.sum(jnp.where(same, pairs, 0.0), axis=1, keepdims=True)
+    wave_rows, quarter_rows = [], []
+    for n in range(chunks * cols // 128):
+        lane = n * 128 + lax.broadcasted_iota(jnp.int32, (1, 128), 1)
+        ch = n * 128 // cols
+        place = ((lane - ch * cols) >> 4) * pair_dev + ch * GROUP + ((lane & 15) >> 2)
+        spot = lax.broadcasted_iota(jnp.int32, (pair_count, 128), 0) == place
+        wave = jnp.sum(jnp.where(spot, pair_column, 0.0), axis=0, keepdims=True)
+        wave_rows.append(jnp.where((lane & 2) == 0, wave, NT - wave))
+        quarter_rows.append(((lane & 1) * (NLON // 4)).astype(jnp.float32))
+
+    def fill_t(kc, _):
+        k_column = (kc * 128 + lax.broadcasted_iota(jnp.int32, (128, 128), 0)).astype(jnp.float32)
+        for n in range(len(wave_rows)):
+            table_t[
+                pl.ds(pl.multiple_of(kc * 128, 128), 128), n * 128 : (n + 1) * 128
+            ] = table_values(wave_rows[n] * k_column + quarter_rows[n])
+        return 0
+
+    lax.fori_loop(0, NLON // 128, fill_t, 0)
+    pick[...] = (
+        (lax.broadcasted_iota(jnp.int32, (NLAT, NLAT), 0) == lat_ref[...])
+        .astype(jnp.float32)
+        .astype(jnp.bfloat16)
+    )
+    means[...] = jnp.zeros_like(means)
+    square = [lax.broadcasted_iota(jnp.int32, (LEV, LEV), n) for n in range(2)]
+    for n in range(STEPS):
+        mix_ref[n] = jnp.where(square[0] == square[1], 0.7, 0.0) + 0.4 * coupling_ref[n]
+
     def chunk_body(ch, _):
         def prepare(s, _):
             slot = ch * GROUP + s
             leg_copy(slot).wait()
-            stored[s] = flat_dot(pick[...], leg_buf[lax.rem(slot, 2)]).astype(jnp.bfloat16)
+            stored[s] = flat_dot(leg_buf[lax.rem(slot, 2)], pick[...]).astype(jnp.bfloat16)
+            spot = lax.broadcasted_iota(jnp.int32, (1, pair_count), 1) == me * pair_dev + slot
+            low_wave = jnp.sum(jnp.where(spot, pairs, 0.0), axis=1, keepdims=True)
+            column = lax.broadcasted_iota(jnp.int32, (1, NT + 2), 1).astype(jnp.float32)
+            second = column >= NT + 1 - low_wave
+            degree = jnp.where(second, column - 1.0, low_wave + column)
+            ratio = degree / NT
+            ratio = ratio * ratio
+            shape_term = degree * (degree + 1.0) / (NT * (NT + 1.0))
+            consts_ref[s, 0:1, :] = second.astype(jnp.float32)
+            consts_ref[s, 1:2, :] = 1.0 / (1.0 + ratio * ratio)
+            for n in range(STEPS):
+                consts_ref[s, 2 + n : 3 + n, :] = 1.0 / (1.0 + damp_ref[n] * shape_term)
+            consts_ref[s, 6:7, :] = jnp.broadcast_to(
+                (low_wave == 0.0).astype(jnp.float32), (1, NT + 2)
+            )
 
             @pl.when(slot + 2 < slots)
             def _():
@@ -438,10 +497,12 @@
                 ],
                 axis=0,
             ).astype(jnp.bfloat16)
-            coeffs = flat_dot(waves_in, stored[s]) * math.sqrt(2.0 / NLAT)
-            second = consts_ref[slot, 0:1, :] > 0.5
+            coeffs = lax.dot_general(
+                waves_in, stored[s], LAST, preferred_element_type=jnp.float32
+            ) * math.sqrt(2.0 / NLAT)
+            second = consts_ref[s, 0:1, :] > 0.5
             incr[s] = (
-                jnp.where(second, coeffs[2 * LEV :], coeffs[: 2 * LEV]) * consts_ref[slot, 1:2, :]
+                jnp.where(second, coeffs[2 * LEV :], coeffs[: 2 * LEV]) * consts_ref[s, 1:2, :]
             )
             spec[s] = back_buf[lax.rem(slot, 2)]
 
@@ -455,10 +516,10 @@
 
         def step(k, _):
             def inverse(s, _):
-                slot = ch * GROUP + s
-                second = consts_ref[slot, 0:1, :] > 0.5
-                inv = consts_ref[slot, pl.ds(2 + k, 1), :]
-                mix = mix_ref[k][:, :LEV]
+                second = consts_ref[s, 0:1, :] > 0.5
+                inv = consts_ref[s, pl.ds(2 + k, 1), :]
+                mix = mix_ref[k]
+                weight = numer_ref[k].astype(jnp.float32) / DEN
                 now = [
                     jnp.dot(
                         mix,
@@ -467,19 +528,17 @@
                         preferred_element_type=jnp.float32,
                     )
                     * inv
-                    + weight_ref[k] * incr[s, r * LEV : (r + 1) * LEV, :]
+                    + weight * incr[s, r * LEV : (r + 1) * LEV, :]
                     for r in range(2)
                 ]
                 for r in range(2):
                     spec[s, r * LEV : (r + 1) * LEV, :] = now[r]
-                means[k] += now[0][:, :128] * consts_ref[slot, 6:7, :128]
+                means[k] += now[0][:, :128] * consts_ref[s, 6:7, :128]
                 both = jnp.concatenate(now, axis=0)
                 split = jnp.concatenate(
                     [jnp.where(second, 0.0, both), jnp.where(second, both, 0.0)], axis=0
                 ).astype(jnp.bfloat16)
-                waves = lax.dot_general(
-                    split, stored[s], LAST, preferred_element_type=jnp.float32
-                ) * math.sqrt(2.0 / NT)
+                waves = flat_dot(split, stored[s]) * math.sqrt(2.0 / NT)
                 for qr in range(4):
                     for t in range(NLAT // 128):
                         turn[t, pl.ds(s * 4 + qr, LEV, stride=rows), :] = waves[
@@ -644,21 +703,21 @@
     level_weight = jnp.where(
         is_level, 1.0 + 2.0 * lane8.astype(jnp.float32) / (LEV - 1), 0.0
     )
-    to_grid = target_ref[1]
-    normaliser = target_ref[2]
+    to_grid = math.sqrt(2.0 / NT) * float(np.float32(math.sqrt(2.0 / NLON)).astype(jnp.bfloat16))
+    lat_sum = sum(math.cos(math.pi * ((n + 0.5) / NLAT - 0.5)) for n in range(NLAT))
+    normaliser = sum(1.0 + 2.0 * n / (LEV - 1) for n in range(LEV)) * lat_sum * NLON
     fix_scale = math.sqrt(NT * NLON) / 2.0
     best = jnp.broadcast_to(best, (8, 128))
     total = jnp.broadcast_to(total, (8, 128))
     base = jnp.broadcast_to(base, (8, 128))
     carried = jnp.zeros((8, 128), jnp.float32)
     shift = carried
-    fixes = carried
     for n in range(STEPS):
         back = (128 - LEV * n) % 128
         best_n, total_n, base_n = [
             pltpu.roll(x, back, 1) if back else x for x in (best, total, base)
         ]
-        column = jnp.sum(mix_ref[n] * carried[0:1], axis=1, keepdims=True)
+        column = jnp.sum(mix_ref[n] * carried[0:1, :LEV], axis=1, keepdims=True)
         moved_by = jnp.broadcast_to(
             jnp.sum(jnp.where(wide_lane == diag, column, 0.0), axis=0, keepdims=True), (8, 128)
         )
@@ -675,9 +734,8 @@
             keepdims=True,
         )
         fix = jnp.log(target_ref[0] / (mass_n / normaliser))
-        fixes = jnp.where(lane8 == n, fix, fixes)
+        fix_ref[n] = fix[0, 0]
         carried = jnp.where(is_level, moved_by + fix * fix_scale, 0.0)
-    fix_ref[...] = fixes
     own = jnp.sum(jnp.where(lane == own_lane, shift[0:1], 0.0), axis=1, keepdims=True)
     shift_ref[...] = jnp.broadcast_to(own, (lev_dev, 128))
 
@@ -687,19 +745,15 @@
     grid_out.wait()
 
 
-def finish_kernel(shift_ref, grid_ref, out_ref):
+def finish_kernel(fix_ref, shift_ref, grid_ref, out_ref, fix_out):
+    for n in range(STEPS):
+        fix_out[n] = fix_ref[n]
     first = pl.program_id(0) * out_ref.shape[0]
     turned = grid_ref[...].T
     for n in range(out_ref.shape[0]):
         out_ref[n, 0] = (
             turned[n * 32 : (n + 1) * 32] + shift_ref[pl.ds(first + n, 1), 0:1]
         ).astype(jnp.bfloat16)
-
-
-def table_factors(wavenumber, quarter, points, axis):
-    phase = (wavenumber * points + quarter) % NLON
-    angle = phase.astype(jnp.float32) * (2.0 * math.pi / NLON)
-    return jnp.cos(angle), jnp.sin(angle)
 
 
 def body(
@@ -732,49 +786,6 @@
             lat_map,
         )
     chunks = pair_dev // GROUP
-    band_id = lax.axis_index("band")
-    lev_id = lax.axis_index("lev")
-
-    low = pair_low.reshape(devs, chunks, GROUP).transpose(1, 0, 2).reshape(-1)
-    column = jnp.arange(4 * low.shape[0], dtype=jnp.int32)
-    wave = jnp.repeat(low, 4)
-    wave = jnp.where(column // 2 % 2 == 0, wave, NT - wave)
-    quarter = column % 2 * (NLON // 4)
-    coarse = jnp.arange(NLON // 128, dtype=jnp.int32) * 128
-    fine = jnp.arange(128, dtype=jnp.int32)
-    norm = math.sqrt(2.0 / NLON)
-    cos_a, sin_a = table_factors(wave[:, None], quarter[:, None], coarse[None, :], 1)
-    cos_b, sin_b = table_factors(wave[:, None], 0, fine[None, :], 1)
-    cos_a, sin_a = cos_a * norm, sin_a * norm
-    cos_at, sin_at = table_factors(wave[None, :], quarter[None, :], coarse[:, None], 0)
-    cos_bt, sin_bt = table_factors(wave[None, :], 0, fine[:, None], 0)
-    cos_at, sin_at = cos_at * norm, sin_at * norm
-
-    local_lats = lax.dynamic_slice_in_dim(lat_map, band_id * lat_dev, lat_dev)
-    row_weight = lat_weights(local_lats).reshape(lat_dev // 32, 1, 32)
-    row_weight = jnp.broadcast_to(row_weight, (lat_dev // 32, lev_dev, 32)).reshape(1, points)
-    own_pairs = lax.dynamic_slice_in_dim(
-        pair_low, (band_id * lev_count + lev_id) * pair_dev, pair_dev
-    )
-    degree, in_second = degrees(own_pairs)
-    holder = jnp.broadcast_to((own_pairs == 0).astype(jnp.float32)[:, None], degree.shape)
-    shape_term = degree * (degree + 1.0) / (NT * (NT + 1.0))
-    consts = jnp.stack(
-        [in_second.astype(jnp.float32), 1.0 / (1.0 + (degree / NT) ** 4)]
-        + [1.0 / (1.0 + damping[n] * shape_term) for n in range(STEPS)]
-        + [holder, holder],
-        axis=1,
-    )
-    eye = jnp.eye(LEV, dtype=jnp.float32)
-    mix = jnp.pad(0.7 * eye + 0.4 * coupling, ((0, 0), (0, 0), (0, 128 - LEV)))
-    all_levels = 1.0 + 2.0 * jnp.arange(LEV, dtype=jnp.float32) / (LEV - 1)
-    normaliser = (
-        jnp.sum(all_levels) * jnp.sum(lat_weights(jnp.arange(NLAT, dtype=jnp.int32))) * NLON
-    )
-    table_entry = jnp.full((), norm, jnp.bfloat16).astype(jnp.float32)
-    scalars = jnp.stack([target_mass[0], math.sqrt(2.0 / NT) * table_entry, normaliser])
-    weights = numerators.astype(jnp.float32) / DEN
-
     vmem = pl.BlockSpec(memory_space=pltpu.VMEM)
     smem = pl.BlockSpec(memory_space=pltpu.SMEM)
     hbm = pl.BlockSpec(memory_space=pl.ANY)
@@ -786,18 +797,20 @@
         ),
         out_shape=(
             jax.ShapeDtypeStruct((NLON, points), jnp.float32),
-            jax.ShapeDtypeStruct((8, 128), jnp.float32),
+            jax.ShapeDtypeStruct((STEPS,), jnp.float32),
             jax.ShapeDtypeStruct((lev_dev, 128), jnp.float32),
         ),
-        in_specs=[smem, smem, hbm, hbm, hbm] + [vmem] * 12,
-        out_specs=(hbm, vmem, vmem),
+        in_specs=[smem] * 3 + [hbm] * 3 + [vmem] * 3,
+        out_specs=(hbm, smem, vmem),
         scratch_shapes=[
+            pltpu.VMEM((GROUP, 8, NT + 2), jnp.float32),
+            pltpu.VMEM((STEPS, LEV, LEV), jnp.float32),
             pltpu.VMEM((points, NLON), jnp.bfloat16),
             pltpu.VMEM((cols, NLON), jnp.bfloat16),
             pltpu.VMEM((NLON, chunks * cols), jnp.bfloat16),
             pltpu.VMEM((NLAT, NLAT), jnp.bfloat16),
-            pltpu.VMEM((2, NLAT, NT + 2), jnp.bfloat16),
-            pltpu.VMEM((GROUP, NLAT, NT + 2), jnp.bfloat16),
+            pltpu.VMEM((2, NT + 2, NLAT), jnp.bfloat16),
+            pltpu.VMEM((GROUP, NT + 2, NLAT), jnp.bfloat16),
             pltpu.VMEM((2, 2 * LEV, NT + 2), jnp.float32),
             pltpu.VMEM((GROUP, 2 * LEV, NT + 2), jnp.float32),
             pltpu.VMEM((GROUP, 2 * LEV, NT + 2), jnp.float32),
@@ -820,38 +833,34 @@
             collective_id=0, has_side_effects=True, vmem_limit_bytes=67043328
         ),
     )(
-        weights,
-        scalars,
+        numerators,
+        damping,
+        target_mass,
         increment,
-        legendre,
+        legendre.transpose(0, 2, 1),
         background.reshape(pair_dev, 2 * LEV, NT + 2),
-        cos_a,
-        sin_a,
-        cos_b,
-        sin_b,
-        cos_at,
-        sin_at,
-        cos_bt,
-        sin_bt,
-        row_weight,
-        lat_map[:, None],
-        consts,
-        mix,
+        pair_low[None, :],
+        lat_map[None, :],
+        coupling,
     )
 
     halves = lev_dev // 4
     splits = lat_dev // 32
-    analysis = pl.pallas_call(
+    analysis, fixes = pl.pallas_call(
         finish_kernel,
         grid=(halves, splits),
         in_specs=[
+            smem,
             pl.BlockSpec((lev_dev, 128), lambda h, j: (0, 0)),
             pl.BlockSpec((NLON, 128), lambda h, j: (0, j * halves + h)),
         ],
-        out_specs=pl.BlockSpec((4, 1, 32, NLON), lambda h, j: (h, j, 0, 0)),
-        out_shape=jax.ShapeDtypeStruct((lev_dev, splits, 32, NLON), jnp.bfloat16),
-    )(shift, grid_t)
-    return (analysis.reshape(lev_dev, lat_dev, NLON), fixes[0, :STEPS])
+        out_specs=(pl.BlockSpec((4, 1, 32, NLON), lambda h, j: (h, j, 0, 0)), smem),
+        out_shape=(
+            jax.ShapeDtypeStruct((lev_dev, splits, 32, NLON), jnp.bfloat16),
+            jax.ShapeDtypeStruct((STEPS,), jnp.float32),
+        ),
+    )(fixes, shift, grid_t)
+    return (analysis.reshape(lev_dev, lat_dev, NLON), fixes)
 
 
 def solution(mesh):

time: 336 us -> 285 us (0.85)
  local copies, waits for them, and re-layouts: 27.9 us -> 2.54 us
  other arithmetic: 19.9 us -> 0 us
  between operations: 5.27 us -> 1.29 us
    unnamed x1 -> x0, local copies, waits for them, and re-layouts: 19.5 us -> none
    sin x2 -> x0, other arithmetic: 9 us -> none  [table_factors(): return (jnp.cos(angle), jnp.sin(angle))]
    mul x4 -> x0, other arithmetic: 4.83 us -> none  [the longest x1 3.64 us: body(): cos_a, sin_a = (cos_a * norm, sin_a * norm)]
where the time goes in v1:
time: 285 us
  Pallas kernels  281 us (99%)
    pallas_call x1, Pallas kernels, body(): pl.pallas_call(lambda *refs: exchange_kernel((band_count, lev_count, lev_...  275 us
    pallas_call x1, Pallas kernels, body(): pl.pallas_call(finish_kernel, grid=(halves, splits), in_specs=[smem, pl.B...  6.14 us

profile of v1, /device:TPU:0, one launch (start us, length us, event | category | flops | bytes accessed | tf_op | source)
XLA Modules:
  0.0 284.7 jit_solution(3449405704262046826)
XLA Ops:
  1.3 1.3 broadcast_in_dim.6.refs_6_
  2.5 1.3 broadcast_in_dim.7.refs_7_
  3.8 274.7 %shard_map.104 = (f32[1536,768]{1,0:T(8,128)}, f32[4]{0:T(128)}, f32[8,128]{1,0:T(8,128)}) custom-call(s32[4]{0:T(128)} %refs_0_.1, f32[4]{0:T(128)} %refs_1_.1, f32[1]{0:T(128)S(6)} %copy.11.refs_2_, bf16[8,96,1536]{2,1,0:T(8,128)(2,1)} %refs_3_.1, bf16[12,769,768]{2,1,0:T(8,128)(2,1)} %bitcast.3, f32[12,64,769]{2,1,0:T(8,128)} %bitcast.4, ...), custom_call_target="tpu_custom_call" | custom-call | tf_op jit(solution)/shard_map/pallas_call | solution.py:794
  278.5 6.1 %shard_map.105 = (bf16[8,3,32,1536]{3,2,1,0:T(8,128)(2,1)}, f32[4]{0:T(128)}) custom-call(f32[4]{0:T(128)} %get-tuple-element.7.fix_ref, f32[8,128]{1,0:T(8,128)} %get-tuple-element.8.shift_ref, f32[1536,768]{1,0:T(8,128)} %get-tuple-element.9.grid_ref), custom_call_target="tpu_custom_call" | custom-call | tf_op jit(solution)/shard_map/pallas_call | solution.py:849

commit v2 on v1

--- a/solution.py
+++ b/solution.py
@@ -223,14 +223,12 @@
     pair_ref,
     lat_ref,
     coupling_ref,
-    grid_ref,
+    out_ref,
     fix_ref,
-    shift_ref,
     consts_ref,
     mix_ref,
     points_in,
     table,
-    table_t,
     pick,
     leg_buf,
     stored,
@@ -242,14 +240,18 @@
     send,
     recv,
     means,
-    stat_send,
-    stat_recv,
+    weight_rows,
+    early_send,
+    early_recv,
+    late_send,
+    late_recv,
     load_sem,
     leg_sem,
     back_sem,
     send_sem,
     recv_sem,
-    stat_sem,
+    early_sem,
+    late_sem,
     out_sem,
 ):
     bands, levs, lev_dev, lat_dev, chunks = sizes
@@ -305,28 +307,35 @@
         leg_copy(slot).start()
         back_copy(slot).start()
 
-    def message(t, o):
-        db, dz = peer(o)
-        return pltpu.make_async_remote_copy(
-            src_ref=send.at[t, pl.ds((db * levs + dz) * rows, rows), :],
-            dst_ref=recv.at[t, pl.ds(me * rows, rows), :],
-            send_sem=send_sem.at[t],
-            recv_sem=recv_sem.at[t],
-            device_id=(db, dz),
-            device_id_type=MESH,
-        )
-
-    def send_all(t):
+    home = pl.ds((lev_id * bands + band_id) * rows, rows)
+
+    def send_level(t, z):
         def one(o, _):
-            message(t, o).start()
+            band = lax.rem(band_id + o, bands)
+            block = send.at[t, pl.ds((z * bands + band) * rows, rows), :]
+            own = jnp.logical_and(o == 0, z == lev_id)
+
+            @pl.when(own)
+            def _():
+                pltpu.make_async_copy(block, recv.at[t, home, :], recv_sem.at[t]).start()
+
+            @pl.when(jnp.logical_not(own))
+            def _():
+                pltpu.make_async_remote_copy(
+                    src_ref=block,
+                    dst_ref=recv.at[t, home, :],
+                    send_sem=send_sem.at[t],
+                    recv_sem=recv_sem.at[t],
+                    device_id=(band, z),
+                    device_id_type=MESH,
+                ).start()
+
             return 0
 
-        lax.fori_loop(1, devs, one, 0)
-        pltpu.make_async_copy(
-            send.at[t, pl.ds(me * rows, rows), :],
-            recv.at[t, pl.ds(me * rows, rows), :],
-            recv_sem.at[t],
-        ).start()
+        lax.fori_loop(0, bands, one, 0)
+
+    def level_order(n):
+        return lax.rem(lev_id + levs // 2 + n, levs)
 
     def wait_recv(t):
         pltpu.make_async_copy(recv.at[t], recv.at[t], recv_sem.at[t]).wait()
@@ -343,7 +352,8 @@
         amount = amount * piece % 128
         return pltpu.roll(x, amount, 1) if amount else x
 
-    lat_now = (lat_ref[...].astype(jnp.float32) + 0.5) / NLAT - 0.5
+    lat_row = lat_ref[...].reshape(1, -1)
+    lat_now = (lat_row.astype(jnp.float32) + 0.5) / NLAT - 0.5
     lat_now = jnp.broadcast_to(sine((0.5 - jnp.abs(lat_now)) * math.pi), (rows, NLAT))
     weight_tiles = []
     for j in range(splits):
@@ -355,72 +365,58 @@
             tile = jnp.where(band_id == b, part, tile)
         weight_tiles += [tile] * halves
     row_weight = jnp.concatenate(weight_tiles, axis=1)[0:1]
-    pairs = pair_ref[...].astype(jnp.float32)
+    pairs = pair_ref[...].reshape(1, -1).astype(jnp.float32)
     pair_count = pairs.shape[1]
     pair_dev = chunks * GROUP
 
-    def fourier(ch, _):
-        def fill(rb, _):
-            col = rb * 128 + lax.broadcasted_iota(jnp.int32, (128, 1), 0)
-            place = (col >> 4) * pair_dev + ch * GROUP + ((col & 15) >> 2)
-            spot = lax.broadcasted_iota(jnp.int32, (128, pair_count), 1) == place
-            wave = jnp.sum(jnp.where(spot, pairs, 0.0), axis=1, keepdims=True)
-            wave = jnp.where((col & 2) == 0, wave, NT - wave)
-            wave = jnp.broadcast_to(wave, (128, 128))
-            quarter = ((col & 1) * (NLON // 4)).astype(jnp.float32)
-            lanes = lax.broadcasted_iota(jnp.int32, (1, 128), 1).astype(jnp.float32)
-            out = pl.multiple_of(rb * 128, 128)
-            for kc in range(NLON // 128):
-                table[pl.ds(out, 128), kc * 128 : (kc + 1) * 128] = table_values(
-                    wave * (lanes + kc * 128.0) + quarter
-                )
-            return 0
-
-        lax.fori_loop(0, cols // 128, fill, 0)
-
-        @pl.when(ch == 0)
+    block_rows = bands * rows
+
+    def fourier(n, _):
+        ch = n // levs
+        z = level_order(lax.rem(n, levs))
+        col = lax.broadcasted_iota(jnp.int32, (block_rows, 1), 0)
+        place = ((col >> 4) * levs + z) * pair_dev + ch * GROUP + ((col & 15) >> 2)
+        spot = lax.broadcasted_iota(jnp.int32, (block_rows, pair_count), 1) == place
+        wave = jnp.sum(jnp.where(spot, pairs, 0.0), axis=1, keepdims=True)
+        wave = jnp.where((col & 2) == 0, wave, NT - wave)
+        wave = jnp.broadcast_to(wave, (block_rows, 128))
+        quarter = ((col & 1) * (NLON // 4)).astype(jnp.float32)
+        lanes = lax.broadcasted_iota(jnp.int32, (1, 128), 1).astype(jnp.float32)
+        at = pl.multiple_of(z * block_rows, block_rows)
+        spot_rows = pl.ds(pl.multiple_of(ch * cols + at, block_rows), block_rows)
+        for kc in range(NLON // 128):
+            table[spot_rows, kc * 128 : (kc + 1) * 128] = table_values(
+                wave * (lanes + kc * 128.0) + quarter
+            )
+
+        @pl.when(n == 0)
         def _():
             pltpu.make_async_copy(points_in, points_in, load_sem).wait()
 
         got = lax.dot_general(
-            table[...], points_in[...], LAST, preferred_element_type=jnp.float32
-        )
-        send[ch] = (got * row_weight).astype(jnp.bfloat16)
-
-        @pl.when(ch == 0)
+            table[spot_rows, :], points_in[...], LAST, preferred_element_type=jnp.float32
+        )
+        send[ch, pl.ds(at, block_rows), :] = (got * row_weight).astype(jnp.bfloat16)
+
+        @pl.when(n == 0)
         def _():
             pl.semaphore_wait(barrier, devs - 1)
 
-        send_all(ch)
+        send_level(ch, z)
         return 0
 
-    lax.fori_loop(0, chunks, fourier, 0)
-
-    same = lax.broadcasted_iota(jnp.int32, (pair_count, pair_count), 0) == (
-        lax.broadcasted_iota(jnp.int32, (pair_count, pair_count), 1)
-    )
-    pair_column = jnp.sum(jnp.where(same, pairs, 0.0), axis=1, keepdims=True)
-    wave_rows, quarter_rows = [], []
-    for n in range(chunks * cols // 128):
-        lane = n * 128 + lax.broadcasted_iota(jnp.int32, (1, 128), 1)
-        ch = n * 128 // cols
-        place = ((lane - ch * cols) >> 4) * pair_dev + ch * GROUP + ((lane & 15) >> 2)
-        spot = lax.broadcasted_iota(jnp.int32, (pair_count, 128), 0) == place
-        wave = jnp.sum(jnp.where(spot, pair_column, 0.0), axis=0, keepdims=True)
-        wave_rows.append(jnp.where((lane & 2) == 0, wave, NT - wave))
-        quarter_rows.append(((lane & 1) * (NLON // 4)).astype(jnp.float32))
-
-    def fill_t(kc, _):
-        k_column = (kc * 128 + lax.broadcasted_iota(jnp.int32, (128, 128), 0)).astype(jnp.float32)
-        for n in range(len(wave_rows)):
-            table_t[
-                pl.ds(pl.multiple_of(kc * 128, 128), 128), n * 128 : (n + 1) * 128
-            ] = table_values(wave_rows[n] * k_column + quarter_rows[n])
-        return 0
-
-    lax.fori_loop(0, NLON // 128, fill_t, 0)
+    lax.fori_loop(0, chunks * levs, fourier, 0)
+
+    lane_at = lax.broadcasted_iota(jnp.int32, (piece, 128), 1)
+    row_at = lax.broadcasted_iota(jnp.int32, (piece, 128), 0)
+    for j in range(splits):
+        lane_weight = row_weight[:, j * lev_dev * piece : j * lev_dev * piece + 128]
+        weight_rows[j] = jnp.broadcast_to(
+            jnp.sum(jnp.where(lane_at == row_at, lane_weight, 0.0), axis=1, keepdims=True),
+            (piece, 128),
+        )
     pick[...] = (
-        (lax.broadcasted_iota(jnp.int32, (NLAT, NLAT), 0) == lat_ref[...])
+        (lax.broadcasted_iota(jnp.int32, (NLAT, NLAT), 0) == lat_row)
         .astype(jnp.float32)
         .astype(jnp.bfloat16)
     )
@@ -470,7 +466,7 @@
                         tiles.append(
                             recv[
                                 ch,
-                                pl.ds(pl.multiple_of((b * levs + z) * rows, rows), rows),
+                                pl.ds(pl.multiple_of((z * bands + b) * rows, rows), rows),
                                 lane0 : lane0 + 128,
                             ].astype(jnp.float32)
                         )
@@ -549,7 +545,8 @@
             lax.fori_loop(0, GROUP, inverse, 0)
             t_out = chunks + ch * STEPS + k
 
-            def depart(z, _):
+            def depart(zi, _):
+                z = level_order(zi)
                 for half in range(halves):
                     for t in range(NLAT // 128):
                         tiles = []
@@ -564,15 +561,15 @@
                             lane0 = (j * halves + half) * 128
                             send[
                                 t_out,
-                                pl.ds(pl.multiple_of((b * levs + z) * rows, rows), rows),
+                                pl.ds(pl.multiple_of((z * bands + b) * rows, rows), rows),
                                 lane0 : lane0 + 128,
                             ] = gather_pieces(
                                 [rolled(tiles[il], il - n) for il in range(per_tile)]
                             ).astype(jnp.bfloat16)
+                send_level(t_out, z)
                 return 0
 
             lax.fori_loop(0, levs, depart, 0)
-            send_all(t_out)
             return 0
 
         lax.fori_loop(0, STEPS, step, 0)
@@ -580,100 +577,210 @@
 
     lax.fori_loop(0, chunks, chunk_body, 0)
 
-    wide = 256
-    sub = lax.broadcasted_iota(jnp.int32, (lev_dev, points), 0)
-    in_level = lax.broadcasted_iota(jnp.int32, (lev_dev, points), 1) // piece % lev_dev == sub
+    tall = lev_dev * piece
     lane = lax.broadcasted_iota(jnp.int32, (lev_dev, 128), 1)
-    own_lane = lev_id * lev_dev + lax.broadcasted_iota(jnp.int32, (lev_dev, 128), 0)
+    level_at = lax.broadcasted_iota(jnp.int32, (lev_dev, 128), 0)
+    half_row = 64
     low = -1e30
 
-    def grid_part(k, lo, hi, add):
-        def part(nb, _):
-            at = pl.ds(pl.multiple_of(nb * wide, wide), wide)
-            total = None
-            for ch in range(lo, hi):
-                one = flat_dot(
-                    table_t[:, ch * cols : (ch + 1) * cols], recv[chunks + ch * STEPS + k, :, at]
-                )
-                total = one if total is None else total + one
-            acc[:, at] = acc[:, at] + total if add else total
+    def grid_block(k, j, lo, hi):
+        at = j * tall if isinstance(j, int) else pl.multiple_of(j * tall, tall)
+        total = None
+        for ch in range(lo, hi):
+            one = flat_dot(
+                recv[chunks + ch * STEPS + k, :, pl.ds(at, tall)].T,
+                table[ch * cols : (ch + 1) * cols, :],
+            )
+            total = one if total is None else total + one
+        return total
+
+    def folded(tile, op):
+        out = tile[:, :128]
+        for n in range(1, NLON // 128):
+            out = op(out, tile[:, n * 128 : (n + 1) * 128])
+        return out
+
+    def mass_block(tile, weights, carry):
+        top, total = carry
+        levels = [tile[n * piece : (n + 1) * piece] for n in range(lev_dev)]
+        block_top = jnp.concatenate(
+            [jnp.max(folded(x, jnp.maximum), axis=0, keepdims=True) for x in levels], axis=0
+        )
+        block_top = jnp.max(block_top, axis=1, keepdims=True)
+        new_top = jnp.maximum(top, jnp.broadcast_to(block_top, top.shape))
+        sums = []
+        for n in range(lev_dev):
+            x = jnp.exp(levels[n] - new_top[n : n + 1, 0:1])
+            sums.append(jnp.sum(folded(x, jnp.add) * weights, axis=0, keepdims=True))
+        block_sum = jnp.sum(jnp.concatenate(sums, axis=0), axis=1, keepdims=True)
+        return new_top, total * jnp.exp(top - new_top) + block_sum
+
+    empty = (
+        jnp.full((lev_dev, 128), low, jnp.float32),
+        jnp.zeros((lev_dev, 128), jnp.float32),
+    )
+
+    def packed_row(carry, base):
+        top, total = carry
+        return jnp.sum(
+            jnp.where(lane == level_at + base, top, 0.0)
+            + jnp.where(lane == level_at + base + half_row, total, 0.0),
+            axis=0,
+            keepdims=True,
+        )
+
+    last = STEPS - 1
+    for ch in range(chunks - 1):
+        wait_recv(chunks + ch * STEPS + last)
+    if chunks > 1:
+
+        def part(j, _):
+            acc[pl.ds(pl.multiple_of(j * tall, tall), tall), :] = grid_block(
+                last, j, 0, chunks - 1
+            )
             return 0
 
-        lax.fori_loop(0, points // wide, part, 0)
-
-    def mass(k, tops_row, sums_row):
-        tops, sums = [], []
-        for nb in range(points // wide):
-            tile = acc[:, nb * wide : (nb + 1) * wide]
-            top = jnp.max(tile, axis=0, keepdims=True)
-            tops.append(top)
-            sums.append(jnp.sum(jnp.exp(tile - top), axis=0, keepdims=True))
-        top = jnp.concatenate(tops, axis=1)
-        total = jnp.concatenate(sums, axis=1) * row_weight
-        level_top = jnp.max(jnp.where(in_level, top, low), axis=1, keepdims=True)
-        level_sum = jnp.sum(
-            jnp.where(in_level, total * jnp.exp(jnp.minimum(top - level_top, 0.0)), 0.0),
-            axis=1,
-            keepdims=True,
-        )
-        here = lane == own_lane + LEV * k
-        tops_row = jnp.where(
-            jnp.max(here.astype(jnp.float32), axis=0, keepdims=True) > 0.5,
-            jnp.sum(jnp.where(here, level_top, 0.0), axis=0, keepdims=True),
-            tops_row,
-        )
-        sums_row = sums_row + jnp.sum(jnp.where(here, level_sum, 0.0), axis=0, keepdims=True)
-        return tops_row, sums_row
-
-    def early(k, carry):
+        lax.fori_loop(0, splits, part, 0)
+
+    def early(k, row):
         def take(ch, _):
             wait_recv(chunks + ch * STEPS + k)
             return 0
 
         lax.fori_loop(0, chunks, take, 0)
-        grid_part(k, 0, chunks, False)
-        return mass(k, *carry)
-
-    rows_now = (jnp.full((1, 128), low, jnp.float32), jnp.zeros((1, 128), jnp.float32))
-    rows_now = lax.fori_loop(0, STEPS - 1, early, rows_now)
-    k = STEPS - 1
-    if chunks > 1:
-        for ch in range(chunks - 1):
-            wait_recv(chunks + ch * STEPS + k)
-        grid_part(k, 0, chunks - 1, False)
-    wait_recv(chunks + (chunks - 1) * STEPS + k)
-    grid_part(k, chunks - 1, chunks, chunks > 1)
-    grid_out = pltpu.make_async_copy(acc, grid_ref, out_sem)
-    grid_out.start()
-    tops_row, sums_row = mass(k, *rows_now)
-
+
+        def part(j, carry):
+            return mass_block(grid_block(k, j, 0, chunks), weight_rows[j], carry)
+
+        return row + packed_row(lax.fori_loop(0, splits, part, empty), k * lev_dev)
+
+    zero_row = jnp.zeros((1, 128), jnp.float32)
+    early_send[0:1, :] = lax.fori_loop(0, last, early, zero_row)
     wide_lane = lax.broadcasted_iota(jnp.int32, (LEV, 128), 1)
     diag = lax.broadcasted_iota(jnp.int32, (LEV, 128), 0)
-    means_row = jnp.zeros((1, 128), jnp.float32)
+    means_row = zero_row
     for n in range(STEPS):
         column = jnp.sum(jnp.where(wide_lane == 0, means[n], 0.0), axis=1, keepdims=True)
         means_row = means_row + jnp.sum(
             jnp.where(wide_lane == diag + LEV * n, column, 0.0), axis=0, keepdims=True
         )
-    stat_send[0:1, :] = tops_row
-    stat_send[1:2, :] = sums_row
-    stat_send[2:3, :] = means_row
-    stat_send[3:4, :] = jnp.zeros((1, 128), jnp.float32)
-
-    def stat_one(o, _):
-        db, dz = peer(o)
-        pltpu.make_async_remote_copy(
-            src_ref=stat_send,
-            dst_ref=stat_recv.at[me],
-            send_sem=stat_sem.at[0],
-            recv_sem=stat_sem.at[1],
-            device_id=(db, dz),
-            device_id_type=MESH,
-        ).start()
-        return 0
-
-    lax.fori_loop(1, devs, stat_one, 0)
-    pltpu.make_async_copy(stat_send, stat_recv.at[me], stat_sem.at[1]).start()
+    early_send[1:2, :] = means_row
+    place_here = lev_id * bands + band_id
+
+    def share(source, target, sems):
+        def one(o, _):
+            db, dz = peer(o)
+            pltpu.make_async_remote_copy(
+                src_ref=source,
+                dst_ref=target.at[place_here],
+                send_sem=sems.at[0],
+                recv_sem=sems.at[1],
+                device_id=(db, dz),
+                device_id_type=MESH,
+            ).start()
+            return 0
+
+        lax.fori_loop(1, devs, one, 0)
+        pltpu.make_async_copy(source, target.at[place_here], sems.at[1]).start()
+
+    def shared(target, sems):
+        pltpu.make_async_copy(target, target, sems.at[1]).wait()
+
+    def sent(target, sems):
+        rest = target.at[pl.ds(0, devs - 1)]
+        pltpu.make_async_copy(rest, rest, sems.at[0]).wait()
+
+    share(early_send, early_recv, early_sem)
+    wait_recv(chunks + (chunks - 1) * STEPS + last)
+    carry = empty
+    for j in range(splits):
+        tile = grid_block(last, j, chunks - 1, chunks)
+        if chunks > 1:
+            tile = tile + acc[j * tall : (j + 1) * tall, :]
+        acc[j * tall : (j + 1) * tall, :] = tile
+        carry = mass_block(tile, weight_rows[j], carry)
+    late_send[0:1, :] = packed_row(carry, 0)
+    share(late_send, late_recv, late_sem)
+
+    row_lane = lax.broadcasted_iota(jnp.int32, (8, 128), 1)
+    to_grid = math.sqrt(2.0 / NT) * float(np.float32(math.sqrt(2.0 / NLON)).astype(jnp.bfloat16))
+    lat_sum = sum(math.cos(math.pi * ((n + 0.5) / NLAT - 0.5)) for n in range(NLAT))
+    normaliser = sum(1.0 + 2.0 * n / (LEV - 1) for n in range(LEV)) * lat_sum * NLON
+    fix_scale = math.sqrt(NT * NLON) / 2.0
+
+    def gathered(target):
+        out = []
+        for z in range(levs):
+            top = target[z * bands, 0:1, :]
+            for b in range(1, bands):
+                top = jnp.maximum(top, target[z * bands + b, 0:1, :])
+            total = zero_row
+            for b in range(bands):
+                here = target[z * bands + b, 0:1, :]
+                total = total + jnp.exp(here - top) * pltpu.roll(
+                    jnp.broadcast_to(here, (8, 128)), 128 - half_row, 1
+                )[0:1]
+            out.append((jnp.broadcast_to(top, (8, 128)), jnp.broadcast_to(total, (8, 128))))
+        return out
+
+    def fix_of(parts, base, shift):
+        valid = jnp.logical_and(row_lane >= base, row_lane < base + lev_dev)
+        total = jnp.zeros((8, 128), jnp.float32)
+        for z in range(levs):
+            turn_by = (base - z * lev_dev) % 128
+            moved = pltpu.roll(shift, turn_by, 1) if turn_by else shift
+            level = (row_lane - base + z * lev_dev).astype(jnp.float32)
+            top, amount = parts[z]
+            total = total + jnp.where(
+                valid,
+                jnp.exp(jnp.where(valid, top + moved, 0.0))
+                * amount
+                * (1.0 + 2.0 * level / (LEV - 1)),
+                0.0,
+            )
+        total = jnp.sum(total, axis=1, keepdims=True)
+        return jnp.log(target_ref[0] / (total / normaliser))
+
+    shared(early_recv, early_sem)
+    parts = gathered(early_recv)
+    base_row = zero_row
+    for d in range(devs):
+        base_row = base_row + early_recv[d, 1:2, :]
+    base_row = jnp.broadcast_to(base_row, (8, 128))
+    is_level = row_lane < LEV
+    carried = jnp.zeros((8, 128), jnp.float32)
+    for n in range(STEPS):
+        back = (128 - LEV * n) % 128
+        base_n = pltpu.roll(base_row, back, 1) if back else base_row
+        column = jnp.sum(mix_ref[n] * carried[0:1, :LEV], axis=1, keepdims=True)
+        moved_by = jnp.broadcast_to(
+            jnp.sum(jnp.where(wide_lane == diag, column, 0.0), axis=0, keepdims=True), (8, 128)
+        )
+        moved = (base_n + moved_by).astype(jnp.bfloat16).astype(jnp.float32) - base_n.astype(
+            jnp.bfloat16
+        ).astype(jnp.float32)
+        shift = jnp.where(is_level, moved * to_grid, 0.0)
+        if n < last:
+            fix = fix_of(parts, n * lev_dev, shift)
+            fix_ref[n] = fix[0, 0]
+            carried = jnp.where(is_level, moved_by + fix * fix_scale, 0.0)
+
+    own_lane = lev_id * lev_dev + level_at
+    own = jnp.sum(jnp.where(lane == own_lane, shift[0:1], 0.0), axis=1, keepdims=True)
+    for j in range(splits):
+        for n in range(lev_dev):
+            here = (j * lev_dev + n) * piece
+            points_in[here : here + piece, :] = (
+                acc[here : here + piece, :] + own[n : n + 1, 0:1]
+            ).astype(jnp.bfloat16)
+            pltpu.make_async_copy(
+                points_in.at[pl.ds(here, piece), :],
+                out_ref.at[n, pl.ds(j * piece, piece), :],
+                out_sem,
+            ).start()
+
+    shared(late_recv, late_sem)
+    fix_ref[last] = fix_of(gathered(late_recv), 0, shift)[0, 0]
 
     def finish(t, _):
         left = send.at[t, pl.ds(0, (devs - 1) * rows), :]
@@ -681,79 +788,9 @@
         return 0
 
     lax.fori_loop(0, chunks * (1 + STEPS), finish, 0)
-    pltpu.make_async_copy(stat_recv, stat_recv, stat_sem.at[1]).wait()
-
-    def find_top(d, best):
-        return jnp.maximum(best, stat_recv[d, 0:1, :])
-
-    best = lax.fori_loop(0, devs, find_top, jnp.full((1, 128), low, jnp.float32))
-
-    def add_up(d, carry):
-        total, base = carry
-        return (
-            total + stat_recv[d, 1:2, :] * jnp.exp(stat_recv[d, 0:1, :] - best),
-            base + stat_recv[d, 2:3, :],
-        )
-
-    zero_row = jnp.zeros((1, 128), jnp.float32)
-    total, base = lax.fori_loop(0, devs, add_up, (zero_row, zero_row))
-
-    lane8 = lax.broadcasted_iota(jnp.int32, (8, 128), 1)
-    is_level = lane8 < LEV
-    level_weight = jnp.where(
-        is_level, 1.0 + 2.0 * lane8.astype(jnp.float32) / (LEV - 1), 0.0
-    )
-    to_grid = math.sqrt(2.0 / NT) * float(np.float32(math.sqrt(2.0 / NLON)).astype(jnp.bfloat16))
-    lat_sum = sum(math.cos(math.pi * ((n + 0.5) / NLAT - 0.5)) for n in range(NLAT))
-    normaliser = sum(1.0 + 2.0 * n / (LEV - 1) for n in range(LEV)) * lat_sum * NLON
-    fix_scale = math.sqrt(NT * NLON) / 2.0
-    best = jnp.broadcast_to(best, (8, 128))
-    total = jnp.broadcast_to(total, (8, 128))
-    base = jnp.broadcast_to(base, (8, 128))
-    carried = jnp.zeros((8, 128), jnp.float32)
-    shift = carried
-    for n in range(STEPS):
-        back = (128 - LEV * n) % 128
-        best_n, total_n, base_n = [
-            pltpu.roll(x, back, 1) if back else x for x in (best, total, base)
-        ]
-        column = jnp.sum(mix_ref[n] * carried[0:1, :LEV], axis=1, keepdims=True)
-        moved_by = jnp.broadcast_to(
-            jnp.sum(jnp.where(wide_lane == diag, column, 0.0), axis=0, keepdims=True), (8, 128)
-        )
-        moved = (base_n + moved_by).astype(jnp.bfloat16).astype(jnp.float32) - base_n.astype(
-            jnp.bfloat16
-        ).astype(jnp.float32)
-        shift = jnp.where(is_level, moved * to_grid, 0.0)
-        mass_n = jnp.sum(
-            jnp.where(
-                is_level, jnp.exp(jnp.where(is_level, best_n + shift, 0.0)) * total_n, 0.0
-            )
-            * level_weight,
-            axis=1,
-            keepdims=True,
-        )
-        fix = jnp.log(target_ref[0] / (mass_n / normaliser))
-        fix_ref[n] = fix[0, 0]
-        carried = jnp.where(is_level, moved_by + fix * fix_scale, 0.0)
-    own = jnp.sum(jnp.where(lane == own_lane, shift[0:1], 0.0), axis=1, keepdims=True)
-    shift_ref[...] = jnp.broadcast_to(own, (lev_dev, 128))
-
-    pltpu.make_async_copy(
-        stat_recv.at[pl.ds(0, devs - 1)], stat_recv.at[pl.ds(0, devs - 1)], stat_sem.at[0]
-    ).wait()
-    grid_out.wait()
-
-
-def finish_kernel(fix_ref, shift_ref, grid_ref, out_ref, fix_out):
-    for n in range(STEPS):
-        fix_out[n] = fix_ref[n]
-    first = pl.program_id(0) * out_ref.shape[0]
-    turned = grid_ref[...].T
-    for n in range(out_ref.shape[0]):
-        out_ref[n, 0] = (
-            turned[n * 32 : (n + 1) * 32] + shift_ref[pl.ds(first + n, 1), 0:1]
-        ).astype(jnp.bfloat16)
+    sent(early_recv, early_sem)
+    sent(late_recv, late_sem)
+    pltpu.make_async_copy(points_in, points_in, out_sem).wait()
 
 
 def body(
@@ -770,6 +807,9 @@
         lat_dev % 32 == 0
         and pair_dev % GROUP == 0
         and lev_dev == 8
+        and band_count * 4 * GROUP == 128
+        and lev_count * lev_dev == LEV
+        and STEPS * lev_dev <= 64
         and points % 256 == 0
         and LEV * STEPS == 128
     )
@@ -791,23 +831,21 @@
     hbm = pl.BlockSpec(memory_space=pl.ANY)
     total = chunks * (1 + STEPS)
     dma = pltpu.SemaphoreType.DMA
-    grid_t, fixes, shift = pl.pallas_call(
+    return pl.pallas_call(
         lambda *refs: exchange_kernel(
             (band_count, lev_count, lev_dev, lat_dev, chunks), *refs
         ),
         out_shape=(
-            jax.ShapeDtypeStruct((NLON, points), jnp.float32),
+            jax.ShapeDtypeStruct((lev_dev, lat_dev, NLON), jnp.bfloat16),
             jax.ShapeDtypeStruct((STEPS,), jnp.float32),
-            jax.ShapeDtypeStruct((lev_dev, 128), jnp.float32),
         ),
         in_specs=[smem] * 3 + [hbm] * 3 + [vmem] * 3,
-        out_specs=(hbm, smem, vmem),
+        out_specs=(hbm, smem),
         scratch_shapes=[
             pltpu.VMEM((GROUP, 8, NT + 2), jnp.float32),
             pltpu.VMEM((STEPS, LEV, LEV), jnp.float32),
             pltpu.VMEM((points, NLON), jnp.bfloat16),
-            pltpu.VMEM((cols, NLON), jnp.bfloat16),
-            pltpu.VMEM((NLON, chunks * cols), jnp.bfloat16),
+            pltpu.VMEM((chunks * cols, NLON), jnp.bfloat16),
             pltpu.VMEM((NLAT, NLAT), jnp.bfloat16),
             pltpu.VMEM((2, NT + 2, NLAT), jnp.bfloat16),
             pltpu.VMEM((GROUP, NT + 2, NLAT), jnp.bfloat16),
@@ -815,17 +853,21 @@
             pltpu.VMEM((GROUP, 2 * LEV, NT + 2), jnp.float32),
             pltpu.VMEM((GROUP, 2 * LEV, NT + 2), jnp.float32),
             pltpu.VMEM((NLAT // 128, LEV * 4 * GROUP, 128), jnp.float32),
-            pltpu.VMEM((NLON, points), jnp.float32),
+            pltpu.VMEM((points, NLON), jnp.float32),
             pltpu.VMEM((total, cols, points), jnp.bfloat16),
             pltpu.VMEM((total, cols, points), jnp.bfloat16),
             pltpu.VMEM((STEPS, LEV, 128), jnp.float32),
-            pltpu.VMEM((4, 128), jnp.float32),
-            pltpu.VMEM((devs, 4, 128), jnp.float32),
+            pltpu.VMEM((lat_dev // 32, 32, 128), jnp.float32),
+            pltpu.VMEM((2, 128), jnp.float32),
+            pltpu.VMEM((devs, 2, 128), jnp.float32),
+            pltpu.VMEM((1, 128), jnp.float32),
+            pltpu.VMEM((devs, 1, 128), jnp.float32),
             dma,
             dma((2,)),
             dma((2,)),
             dma((total,)),
             dma((total,)),
+            dma((2,)),
             dma((2,)),
             dma,
         ],
@@ -839,28 +881,10 @@
         increment,
         legendre.transpose(0, 2, 1),
         background.reshape(pair_dev, 2 * LEV, NT + 2),
-        pair_low[None, :],
-        lat_map[None, :],
+        pair_low,
+        lat_map,
         coupling,
     )
-
-    halves = lev_dev // 4
-    splits = lat_dev // 32
-    analysis, fixes = pl.pallas_call(
-        finish_kernel,
-        grid=(halves, splits),
-        in_specs=[
-            smem,
-            pl.BlockSpec((lev_dev, 128), lambda h, j: (0, 0)),
-            pl.BlockSpec((NLON, 128), lambda h, j: (0, j * halves + h)),
-        ],
-        out_specs=(pl.BlockSpec((4, 1, 32, NLON), lambda h, j: (h, j, 0, 0)), smem),
-        out_shape=(
-            jax.ShapeDtypeStruct((lev_dev, splits, 32, NLON), jnp.bfloat16),
-            jax.ShapeDtypeStruct((STEPS,), jnp.float32),
-        ),
-    )(fixes, shift, grid_t)
-    return (analysis.reshape(lev_dev, lat_dev, NLON), fixes)
 
 
 def solution(mesh):

time: 285 us -> 277 us (0.972)
  Pallas kernels: 281 us -> 272 us
    pallas_call x1 -> x0, Pallas kernels: 6.14 us -> none  [body(): pl.pallas_call(finish_kernel, grid=(halves, splits), in_specs=[smem, pl.B...]
    unnamed x0 -> x4, local copies, waits for them, and re-layouts: none -> 3.74 us
    pallas_call x1, Pallas kernels: 275 us -> 272 us  [body(): pl.pallas_call(lambda *refs: exchange_kernel((band_count, lev_count, lev_...]
where the time goes in v2:
time: 277 us
  Pallas kernels  272 us (98%)
  local copies, waits for them, and re-layouts  3.74 us (1%)
    pallas_call x1, Pallas kernels, body(): pl.pallas_call(lambda *refs: exchange_kernel((band_count, lev_count, lev_...  272 us

profile of v2, /device:TPU:0, one launch (start us, length us, event | category | flops | bytes accessed | tf_op | source)
XLA Modules:
  0.0 276.7 jit_solution(8948974235101293227)
XLA Ops:
  1.3 271.7 %shard_map.104 = (bf16[8,96,1536]{2,1,0:T(8,128)(2,1)}, f32[4]{0:T(128)}) custom-call(s32[4]{0:T(128)} %refs_0_.1, f32[4]{0:T(128)} %refs_1_.1, f32[1]{0:T(128)S(6)} %copy.13.refs_2_, bf16[8,96,1536]{2,1,0:T(8,128)(2,1)} %refs_3_.1, bf16[12,769,768]{2,1,0:T(8,128)(2,1)} %bitcast.2, f32[12,64,769]{2,1,0:T(8,128)} %bitcast.3, s32[384]{0:T(512)} %refs_6_.1, ...), custom_call_target="tpu_custom_call" | custom-call | tf_op jit(solution)/shard_map/pallas_call | solution.py:834
  273.0 0.0 copy-start
  273.0 3.2 %copy.14 = bf16[8,96,1536]{2,1,0:T(8,128)(2,1)} copy(bf16[8,96,1536]{2,1,0:T(8,128)(2,1)} %get-tuple-element.4) | data formatting | bytes 4718592
  276.2 0.0 copy-done
  276.2 0.5 copy.15
Async XLA Ops:
  273.0 3.2 %copy-start = (f32[4]{0:T(128)S(1)}, f32[4]{0:T(128)}, u32[]{:S(2)}) copy-start(f32[4]{0:T(128)} %get-tuple-element.5) | copy-start | bytes 52

commit v3 on v2

--- a/solution.py
+++ b/solution.py
@@ -250,9 +250,9 @@
     back_sem,
     send_sem,
     recv_sem,
+    piece_sem,
     early_sem,
     late_sem,
-    out_sem,
 ):
     bands, levs, lev_dev, lat_dev, chunks = sizes
     devs = bands * levs
@@ -333,6 +333,40 @@
             return 0
 
         lax.fori_loop(0, bands, one, 0)
+
+    final = chunks * (1 + STEPS) - 1
+    tall = lev_dev * piece
+
+    def send_pieces():
+        def one(n, _):
+            j = n // devs
+            o = lax.rem(n, bands)
+            z = level_order(lax.rem(n // bands, levs))
+            band = lax.rem(band_id + o, bands)
+            lanes = pl.ds(pl.multiple_of(j * tall, tall), tall)
+            block = send.at[final, pl.ds((z * bands + band) * rows, rows), lanes]
+            own = jnp.logical_and(o == 0, z == lev_id)
+
+            @pl.when(own)
+            def _():
+                pltpu.make_async_copy(
+                    block, recv.at[final, home, lanes], piece_sem.at[j]
+                ).start()
+
+            @pl.when(jnp.logical_not(own))
+            def _():
+                pltpu.make_async_remote_copy(
+                    src_ref=block,
+                    dst_ref=recv.at[final, home, lanes],
+                    send_sem=send_sem.at[final],
+                    recv_sem=piece_sem.at[j],
+                    device_id=(band, z),
+                    device_id_type=MESH,
+                ).start()
+
+            return 0
+
+        lax.fori_loop(0, splits * devs, one, 0)
 
     def level_order(n):
         return lax.rem(lev_id + levs // 2 + n, levs)
@@ -566,10 +600,19 @@
                             ] = gather_pieces(
                                 [rolled(tiles[il], il - n) for il in range(per_tile)]
                             ).astype(jnp.bfloat16)
-                send_level(t_out, z)
+
+                @pl.when(t_out != final)
+                def _():
+                    send_level(t_out, z)
+
                 return 0
 
             lax.fori_loop(0, levs, depart, 0)
+
+            @pl.when(t_out == final)
+            def _():
+                send_pieces()
+
             return 0
 
         lax.fori_loop(0, STEPS, step, 0)
@@ -577,7 +620,6 @@
 
     lax.fori_loop(0, chunks, chunk_body, 0)
 
-    tall = lev_dev * piece
     lane = lax.broadcasted_iota(jnp.int32, (lev_dev, 128), 1)
     level_at = lax.broadcasted_iota(jnp.int32, (lev_dev, 128), 0)
     half_row = 64
@@ -691,9 +733,10 @@
         pltpu.make_async_copy(rest, rest, sems.at[0]).wait()
 
     share(early_send, early_recv, early_sem)
-    wait_recv(chunks + (chunks - 1) * STEPS + last)
     carry = empty
     for j in range(splits):
+        arrived = recv.at[final, :, pl.ds(j * tall, tall)]
+        pltpu.make_async_copy(arrived, arrived, piece_sem.at[j]).wait()
         tile = grid_block(last, j, chunks - 1, chunks)
         if chunks > 1:
             tile = tile + acc[j * tall : (j + 1) * tall, :]
@@ -770,14 +813,9 @@
     for j in range(splits):
         for n in range(lev_dev):
             here = (j * lev_dev + n) * piece
-            points_in[here : here + piece, :] = (
+            out_ref[n, j * piece : (j + 1) * piece, :] = (
                 acc[here : here + piece, :] + own[n : n + 1, 0:1]
             ).astype(jnp.bfloat16)
-            pltpu.make_async_copy(
-                points_in.at[pl.ds(here, piece), :],
-                out_ref.at[n, pl.ds(j * piece, piece), :],
-                out_sem,
-            ).start()
 
     shared(late_recv, late_sem)
     fix_ref[last] = fix_of(gathered(late_recv), 0, shift)[0, 0]
@@ -790,7 +828,6 @@
     lax.fori_loop(0, chunks * (1 + STEPS), finish, 0)
     sent(early_recv, early_sem)
     sent(late_recv, late_sem)
-    pltpu.make_async_copy(points_in, points_in, out_sem).wait()
 
 
 def body(
@@ -836,11 +873,11 @@
             (band_count, lev_count, lev_dev, lat_dev, chunks), *refs
         ),
         out_shape=(
-            jax.ShapeDtypeStruct((lev_dev, lat_dev, NLON), jnp.bfloat16),
+            pltpu.VMEM((lev_dev, lat_dev, NLON), jnp.bfloat16),
             jax.ShapeDtypeStruct((STEPS,), jnp.float32),
         ),
         in_specs=[smem] * 3 + [hbm] * 3 + [vmem] * 3,
-        out_specs=(hbm, smem),
+        out_specs=(vmem, smem),
         scratch_shapes=[
             pltpu.VMEM((GROUP, 8, NT + 2), jnp.float32),
             pltpu.VMEM((STEPS, LEV, LEV), jnp.float32),
@@ -867,12 +904,12 @@
             dma((2,)),
             dma((total,)),
             dma((total,)),
+            dma((lat_dev // 32,)),
             dma((2,)),
             dma((2,)),
-            dma,
         ],
         compiler_params=pltpu.CompilerParams(
-            collective_id=0, has_side_effects=True, vmem_limit_bytes=67043328
+            collective_id=0, has_side_effects=True, vmem_limit_bytes=62000000
         ),
     )(
         numerators,

time: 277 us -> 274 us (0.989)
  no operation moved by 1% of the time
where the time goes in v3:
time: 274 us
  Pallas kernels  271 us (99%)
    pallas_call x1, Pallas kernels, body(): pl.pallas_call(lambda *refs: exchange_kernel((band_count, lev_count, lev_...  271 us

profile of v3, /device:TPU:0, one launch (start us, length us, event | category | flops | bytes accessed | tf_op | source)
XLA Modules:
  0.0 273.8 jit_solution(12537024809221816187)
XLA Ops:
  1.3 270.6 %shard_map.104 = (bf16[8,96,1536]{2,1,0:T(8,128)(2,1)S(1)}, f32[4]{0:T(128)}) custom-call(s32[4]{0:T(128)} %refs_0_.1, f32[4]{0:T(128)} %refs_1_.1, f32[1]{0:T(128)S(6)} %copy.14.refs_2_, bf16[8,96,1536]{2,1,0:T(8,128)(2,1)} %refs_3_.1, bf16[12,769,768]{2,1,0:T(8,128)(2,1)} %bitcast.2, f32[12,64,769]{2,1,0:T(8,128)} %bitcast.3, s32[384]{0:T(512)} %refs_6_.1, ...), custom_call_target="tpu_custom_call" | custom-call | tf_op jit(solution)/shard_map/pallas_call | solution.py:871
  271.9 0.0 copy-start
  271.9 1.4 copy.13
  273.3 0.0 copy-done
  273.3 0.5 copy.15
Async XLA Ops:
  271.9 1.4 copy-start

commit v4 on v3

--- a/solution.py
+++ b/solution.py
@@ -214,17 +214,24 @@
 
 def exchange_kernel(
     sizes,
+    numer_in,
+    damp_in,
+    target_in,
+    inc_ref,
+    leg_ref,
+    back_ref,
+    pair_in,
+    lat_in,
+    coupling_in,
+    out_ref,
+    fix_ref,
     numer_ref,
     damp_ref,
     target_ref,
-    inc_ref,
-    leg_ref,
-    back_ref,
     pair_ref,
     lat_ref,
     coupling_ref,
-    out_ref,
-    fix_ref,
+    small_sem,
     consts_ref,
     mix_ref,
     points_in,
@@ -282,6 +289,22 @@
 
     lax.fori_loop(1, devs, greet, 0)
 
+    small = [
+        pltpu.make_async_copy(source, target, small_sem.at[n])
+        for n, (source, target) in enumerate(
+            [
+                (pair_in, pair_ref),
+                (lat_in, lat_ref),
+                (coupling_in, coupling_ref),
+                (numer_in, numer_ref),
+                (damp_in, damp_ref),
+                (target_in, target_ref),
+            ]
+        )
+    ]
+    for copy in small:
+        copy.start()
+
     def load_piece(i, j):
         return pltpu.make_async_copy(
             inc_ref.at[i, pl.ds(j * piece, piece), :],
@@ -343,7 +366,7 @@
             o = lax.rem(n, bands)
             z = level_order(lax.rem(n // bands, levs))
             band = lax.rem(band_id + o, bands)
-            lanes = pl.ds(pl.multiple_of(j * tall, tall), tall)
+            lanes = pl.ds(pl.multiple_of(j * 128, 128), 128)
             block = send.at[final, pl.ds((z * bands + band) * rows, rows), lanes]
             own = jnp.logical_and(o == 0, z == lev_id)
 
@@ -366,7 +389,7 @@
 
             return 0
 
-        lax.fori_loop(0, splits * devs, one, 0)
+        lax.fori_loop(0, splits * halves * devs, one, 0)
 
     def level_order(n):
         return lax.rem(lev_id + levs // 2 + n, levs)
@@ -386,6 +409,8 @@
         amount = amount * piece % 128
         return pltpu.roll(x, amount, 1) if amount else x
 
+    small[0].wait()
+    small[1].wait()
     lat_row = lat_ref[...].reshape(1, -1)
     lat_now = (lat_row.astype(jnp.float32) + 0.5) / NLAT - 0.5
     lat_now = jnp.broadcast_to(sine((0.5 - jnp.abs(lat_now)) * math.pi), (rows, NLAT))
@@ -455,6 +480,8 @@
         .astype(jnp.bfloat16)
     )
     means[...] = jnp.zeros_like(means)
+    for copy in small[2:]:
+        copy.wait()
     square = [lax.broadcasted_iota(jnp.int32, (LEV, LEV), n) for n in range(2)]
     for n in range(STEPS):
         mix_ref[n] = jnp.where(square[0] == square[1], 0.7, 0.0) + 0.4 * coupling_ref[n]
@@ -601,36 +628,38 @@
                                 [rolled(tiles[il], il - n) for il in range(per_tile)]
                             ).astype(jnp.bfloat16)
 
-                @pl.when(t_out != final)
+                @pl.when(k != STEPS - 1)
                 def _():
                     send_level(t_out, z)
 
                 return 0
 
             lax.fori_loop(0, levs, depart, 0)
-
-            @pl.when(t_out == final)
-            def _():
-                send_pieces()
-
             return 0
 
         lax.fori_loop(0, STEPS, step, 0)
         return 0
 
     lax.fori_loop(0, chunks, chunk_body, 0)
+
+    def send_last(n, _):
+        send_level(chunks + n // levs * STEPS + STEPS - 1, level_order(lax.rem(n, levs)))
+        return 0
+
+    lax.fori_loop(0, (chunks - 1) * levs, send_last, 0)
 
     lane = lax.broadcasted_iota(jnp.int32, (lev_dev, 128), 1)
     level_at = lax.broadcasted_iota(jnp.int32, (lev_dev, 128), 0)
     half_row = 64
     low = -1e30
 
-    def grid_block(k, j, lo, hi):
-        at = j * tall if isinstance(j, int) else pl.multiple_of(j * tall, tall)
+    def grid_block(k, j, lo, hi, size=None):
+        size = size or tall
+        at = j * size if isinstance(j, int) else pl.multiple_of(j * size, size)
         total = None
         for ch in range(lo, hi):
             one = flat_dot(
-                recv[chunks + ch * STEPS + k, :, pl.ds(at, tall)].T,
+                recv[chunks + ch * STEPS + k, :, pl.ds(at, size)].T,
                 table[ch * cols : (ch + 1) * cols, :],
             )
             total = one if total is None else total + one
@@ -644,14 +673,15 @@
 
     def mass_block(tile, weights, carry):
         top, total = carry
-        levels = [tile[n * piece : (n + 1) * piece] for n in range(lev_dev)]
+        count = tile.shape[0] // piece
+        levels = [tile[n * piece : (n + 1) * piece] for n in range(count)]
         block_top = jnp.concatenate(
             [jnp.max(folded(x, jnp.maximum), axis=0, keepdims=True) for x in levels], axis=0
         )
         block_top = jnp.max(block_top, axis=1, keepdims=True)
         new_top = jnp.maximum(top, jnp.broadcast_to(block_top, top.shape))
         sums = []
-        for n in range(lev_dev):
+        for n in range(count):
             x = jnp.exp(levels[n] - new_top[n : n + 1, 0:1])
             sums.append(jnp.sum(folded(x, jnp.add) * weights, axis=0, keepdims=True))
         block_sum = jnp.sum(jnp.concatenate(sums, axis=0), axis=1, keepdims=True)
@@ -672,18 +702,6 @@
         )
 
     last = STEPS - 1
-    for ch in range(chunks - 1):
-        wait_recv(chunks + ch * STEPS + last)
-    if chunks > 1:
-
-        def part(j, _):
-            acc[pl.ds(pl.multiple_of(j * tall, tall), tall), :] = grid_block(
-                last, j, 0, chunks - 1
-            )
-            return 0
-
-        lax.fori_loop(0, splits, part, 0)
-
     def early(k, row):
         def take(ch, _):
             wait_recv(chunks + ch * STEPS + k)
@@ -733,17 +751,18 @@
         pltpu.make_async_copy(rest, rest, sems.at[0]).wait()
 
     share(early_send, early_recv, early_sem)
-    carry = empty
-    for j in range(splits):
-        arrived = recv.at[final, :, pl.ds(j * tall, tall)]
-        pltpu.make_async_copy(arrived, arrived, piece_sem.at[j]).wait()
-        tile = grid_block(last, j, chunks - 1, chunks)
-        if chunks > 1:
-            tile = tile + acc[j * tall : (j + 1) * tall, :]
-        acc[j * tall : (j + 1) * tall, :] = tile
-        carry = mass_block(tile, weight_rows[j], carry)
-    late_send[0:1, :] = packed_row(carry, 0)
-    share(late_send, late_recv, late_sem)
+    send_pieces()
+    for ch in range(chunks - 1):
+        wait_recv(chunks + ch * STEPS + last)
+    if chunks > 1:
+
+        def part(j, _):
+            acc[pl.ds(pl.multiple_of(j * tall, tall), tall), :] = grid_block(
+                last, j, 0, chunks - 1
+            )
+            return 0
+
+        lax.fori_loop(0, splits, part, 0)
 
     row_lane = lax.broadcasted_iota(jnp.int32, (8, 128), 1)
     to_grid = math.sqrt(2.0 / NT) * float(np.float32(math.sqrt(2.0 / NLON)).astype(jnp.bfloat16))
@@ -754,15 +773,11 @@
     def gathered(target):
         out = []
         for z in range(levs):
-            top = target[z * bands, 0:1, :]
-            for b in range(1, bands):
-                top = jnp.maximum(top, target[z * bands + b, 0:1, :])
-            total = zero_row
-            for b in range(bands):
-                here = target[z * bands + b, 0:1, :]
-                total = total + jnp.exp(here - top) * pltpu.roll(
-                    jnp.broadcast_to(here, (8, 128)), 128 - half_row, 1
-                )[0:1]
+            here = target[z * bands : (z + 1) * bands, 0, :]
+            top = jnp.max(here, axis=0, keepdims=True)
+            total = jnp.sum(
+                jnp.exp(here - top) * pltpu.roll(here, 128 - half_row, 1), axis=0, keepdims=True
+            )
             out.append((jnp.broadcast_to(top, (8, 128)), jnp.broadcast_to(total, (8, 128))))
         return out
 
@@ -787,8 +802,10 @@
     shared(early_recv, early_sem)
     parts = gathered(early_recv)
     base_row = zero_row
-    for d in range(devs):
-        base_row = base_row + early_recv[d, 1:2, :]
+    for z in range(levs):
+        base_row = base_row + jnp.sum(
+            early_recv[z * bands : (z + 1) * bands, 1, :], axis=0, keepdims=True
+        )
     base_row = jnp.broadcast_to(base_row, (8, 128))
     is_level = row_lane < LEV
     carried = jnp.zeros((8, 128), jnp.float32)
@@ -810,12 +827,23 @@
 
     own_lane = lev_id * lev_dev + level_at
     own = jnp.sum(jnp.where(lane == own_lane, shift[0:1], 0.0), axis=1, keepdims=True)
-    for j in range(splits):
-        for n in range(lev_dev):
-            here = (j * lev_dev + n) * piece
-            out_ref[n, j * piece : (j + 1) * piece, :] = (
-                acc[here : here + piece, :] + own[n : n + 1, 0:1]
+    carries = [tuple(x[:per_tile] for x in empty)] * halves
+    for n in range(splits * halves):
+        here = slice(n * 128, (n + 1) * 128)
+        arrived = recv.at[final, :, here]
+        pltpu.make_async_copy(arrived, arrived, piece_sem.at[n]).wait()
+        tile = grid_block(last, n, chunks - 1, chunks, 128)
+        if chunks > 1:
+            tile = tile + acc[here, :]
+        for m in range(per_tile):
+            level = n % halves * per_tile + m
+            out_ref[level, n // halves * piece : (n // halves + 1) * piece, :] = (
+                tile[m * piece : (m + 1) * piece] + own[level : level + 1, 0:1]
             ).astype(jnp.bfloat16)
+        carries[n % halves] = mass_block(tile, weight_rows[n // halves], carries[n % halves])
+    carry = tuple(jnp.concatenate([c[n] for c in carries], axis=0) for n in range(2))
+    late_send[0:1, :] = packed_row(carry, 0)
+    share(late_send, late_recv, late_sem)
 
     shared(late_recv, late_sem)
     fix_ref[last] = fix_of(gathered(late_recv), 0, shift)[0, 0]
@@ -876,9 +904,16 @@
             pltpu.VMEM((lev_dev, lat_dev, NLON), jnp.bfloat16),
             jax.ShapeDtypeStruct((STEPS,), jnp.float32),
         ),
-        in_specs=[smem] * 3 + [hbm] * 3 + [vmem] * 3,
+        in_specs=[hbm] * 9,
         out_specs=(vmem, smem),
         scratch_shapes=[
+            pltpu.SMEM((STEPS,), jnp.int32),
+            pltpu.SMEM((STEPS,), jnp.float32),
+            pltpu.SMEM((1,), jnp.float32),
+            pltpu.VMEM(pair_low.shape, jnp.int32),
+            pltpu.VMEM(lat_map.shape, jnp.int32),
+            pltpu.VMEM(coupling.shape, jnp.float32),
+            pltpu.SemaphoreType.DMA((6,)),
             pltpu.VMEM((GROUP, 8, NT + 2), jnp.float32),
             pltpu.VMEM((STEPS, LEV, LEV), jnp.float32),
             pltpu.VMEM((points, NLON), jnp.bfloat16),
@@ -904,7 +939,7 @@
             dma((2,)),
             dma((total,)),
             dma((total,)),
-            dma((lat_dev // 32,)),
+            dma((points // 128,)),
             dma((2,)),
             dma((2,)),
         ],

time: 274 us -> 274 us (level)
  no operation moved by 1% of the time
where the time goes in v4:
time: 274 us; the launch traced here: 273 us
  Pallas kernels  270 us (99%)
    pallas_call x1, Pallas kernels, body(): pl.pallas_call(lambda *refs: exchange_kernel((band_count, lev_count, lev_...  270 us

profile of v4, /device:TPU:0, one launch (start us, length us, event | category | flops | bytes accessed | tf_op | source)
XLA Modules:
  0.0 273.2 jit_solution(12026517744652086068)
XLA Ops:
  1.3 270.0 %shard_map.104 = (bf16[8,96,1536]{2,1,0:T(8,128)(2,1)S(1)}, f32[4]{0:T(128)}) custom-call(s32[4]{0:T(128)} %refs_0_.1, f32[4]{0:T(128)} %refs_1_.1, f32[1]{0:T(128)S(6)} %copy.14.refs_2_, bf16[8,96,1536]{2,1,0:T(8,128)(2,1)} %refs_3_.1, bf16[12,769,768]{2,1,0:T(8,128)(2,1)} %bitcast.2, f32[12,64,769]{2,1,0:T(8,128)} %bitcast.3, s32[384]{0:T(512)} %refs_6_.1, ...), custom_call_target="tpu_custom_call" | custom-call | tf_op jit(solution)/shard_map/pallas_call | solution.py:899
  271.3 0.0 copy-start
  271.3 1.4 copy.13
  272.7 0.0 copy-done
  272.7 0.5 copy.15
Async XLA Ops:
  271.3 1.4 copy-start

commit v5 on v4

--- a/solution.py
+++ b/solution.py
@@ -845,9 +845,6 @@
     late_send[0:1, :] = packed_row(carry, 0)
     share(late_send, late_recv, late_sem)
 
-    shared(late_recv, late_sem)
-    fix_ref[last] = fix_of(gathered(late_recv), 0, shift)[0, 0]
-
     def finish(t, _):
         left = send.at[t, pl.ds(0, (devs - 1) * rows), :]
         pltpu.make_async_copy(left, left, send_sem.at[t]).wait()
@@ -855,6 +852,9 @@
 
     lax.fori_loop(0, chunks * (1 + STEPS), finish, 0)
     sent(early_recv, early_sem)
+    shared(late_recv, late_sem)
+    fix_ref[last] = fix_of(gathered(late_recv), 0, shift)[0, 0]
+
     sent(late_recv, late_sem)
 
 

time: 274 us -> 273 us (level)
  no operation moved by 1% of the time
where the time goes in v5:
time: 273 us
  Pallas kernels  270 us (99%)
    pallas_call x1, Pallas kernels, body(): pl.pallas_call(lambda *refs: exchange_kernel((band_count, lev_count, lev_...  270 us

profile of v5, /device:TPU:0, one launch (start us, length us, event | category | flops | bytes accessed | tf_op | source)
XLA Modules:
  0.0 273.1 jit_solution(3516633009126712551)
XLA Ops:
  1.3 269.9 %shard_map.104 = (bf16[8,96,1536]{2,1,0:T(8,128)(2,1)S(1)}, f32[4]{0:T(128)}) custom-call(s32[4]{0:T(128)} %refs_0_.1, f32[4]{0:T(128)} %refs_1_.1, f32[1]{0:T(128)S(6)} %copy.14.refs_2_, bf16[8,96,1536]{2,1,0:T(8,128)(2,1)} %refs_3_.1, bf16[12,769,768]{2,1,0:T(8,128)(2,1)} %bitcast.2, f32[12,64,769]{2,1,0:T(8,128)} %bitcast.3, s32[384]{0:T(512)} %refs_6_.1, ...), custom_call_target="tpu_custom_call" | custom-call | tf_op jit(solution)/shard_map/pallas_call | solution.py:899
  271.2 0.0 copy-start
  271.2 1.4 copy.13
  272.6 0.0 copy-done
  272.6 0.5 copy.15
Async XLA Ops:
  271.2 1.4 copy-start
